TPU v7x, 32 devices: a whole 2x2x4 slice. The times are simulated.
32 devices in a mesh: seq: 4 (over y, x), exp: 8 (over z, core).
Axes of the slice: x: 2, y: 2, z: 4, core: 2. Of those that a mesh axis runs over, the one named last changes fastest.
Arguments:
- queries: bfloat16 [4096, 3072], P(('seq', 'exp')), may hold values from -123 to 123
- keys: bfloat16 [4096, 512], P(('seq', 'exp')), may hold values from -6 to 6
- values: bfloat16 [4096, 512], P(('seq', 'exp')), may hold values from -9 to 9
- residual: bfloat16 [4096, 6144], P(('seq', 'exp')), may hold values from -51 to 51
- proj_weight: bfloat16 [3072, 6144], P('seq', 'exp'), may hold values from -0.109375 to 0.109375
- norm_gain: bfloat16 [6144], replicated, may hold values from 0.099609375 to 1.8984375
- router: bfloat16 [6144, 8], replicated, may hold values from -0.078125 to 0.078125
- expert_ids: int32 [4096, 2], P(('seq', 'exp')), may hold values from 0 to 7, all different within a row; in each aligned block of 128 rows (0 to 127, 128 to 255, ...) at most 33 rows name the same one
- u_gate_up: bfloat16 [8, 6144, 1024], P('exp'), may hold values from -0.078125 to 0.078125
- v_gate_up: bfloat16 [8, 2, 512, 8192], P('exp'), may hold values from -0.25 to 0.25
- u_down: bfloat16 [8, 8192, 512], P('exp'), may hold values from -0.0625 to 0.0625
- v_down: bfloat16 [8, 512, 6144], P('exp'), may hold values from -0.25 to 0.25
Outputs:
- layer_out: bfloat16 [4096, 6144], P(('seq', 'exp'))
Inputs may be any that keep to these rules, and one draw needn't show every extreme that they name: `expert_ids`: the two experts of a token differ. Among the tokens of one device no expert is named more than 33 times, and in some devices' tokens some expert is named exactly 33 times.
All inputs are finite; a program needn't handle non-finite values.
Results may differ from a plain program's by a relative error of at most 0.02.
Values may be sent and summed in bfloat16 or wider, within the bound.
A program may use at most 192 MiB of HBM per device.

v0:
```python
import functools

import jax
import jax.numpy as jnp
from jax import lax
from jax.experimental import pallas as pl
from jax.experimental.pallas import tpu as pltpu
from jax.sharding import PartitionSpec as P

D = 6144
HEADS = 24
KV_HEADS = 4
HEAD_DIM = 128
EXPERTS = 8
RANK = 512
TOK_DEV = 128
CAP = 33


EPS = 1e-05
LOG2_E = 1.4426950408889634


def swapped(x, axis, distance):
    return lax.ppermute(x, axis, [(i, i ^ 1 << distance) for i in range(lax.axis_size(axis))])


def attention_kernel(heads, parts, q_ref, kv_ref, out_ref):
    block = pl.program_id(0)
    column = lax.axis_index("exp")
    columns = kv_ref.shape[0]
    span = columns // parts
    chunk = span * TOK_DEV
    rows = heads * TOK_DEV
    query = jnp.concatenate(
        [q_ref[:, h * HEAD_DIM : (h + 1) * HEAD_DIM] for h in range(heads)], axis=0
    )

    def step(index, carried, masked):
        row_max, row_sum, weighted = carried
        held = kv_ref[pl.ds((index % parts) * span, span), index // parts]
        held = held.reshape(chunk, 2 * HEAD_DIM)
        scores = lax.dot_general(
            query, held[:, :HEAD_DIM], (((1,), (1,)), ((), ())), preferred_element_type=jnp.float32
        ) * (HEAD_DIM ** (-0.5) * LOG2_E)
        if masked:
            offset = (column % span) * TOK_DEV
            own = lax.broadcasted_iota(jnp.int32, (rows, chunk), 0) % TOK_DEV + offset
            other = lax.broadcasted_iota(jnp.int32, (rows, chunk), 1)
            scores = jnp.where(other <= own, scores, -jnp.inf)
        new_max = jnp.maximum(row_max, jnp.max(scores, axis=-1, keepdims=True))
        fading = jnp.exp2(row_max - new_max)
        terms = jnp.exp2(scores - new_max)
        row_sum = row_sum * fading + jnp.sum(terms, axis=-1, keepdims=True)
        update = jnp.dot(
            terms.astype(jnp.bfloat16), held[:, HEAD_DIM:], preferred_element_type=jnp.float32
        )
        return new_max, row_sum, weighted * fading + update

    carried = (
        jnp.full((rows, 1), -1e30, jnp.float32),
        jnp.zeros((rows, 1), jnp.float32),
        jnp.zeros((rows, HEAD_DIM), jnp.float32),
    )
    last = block * parts + column // span
    carried = lax.fori_loop(0, last, lambda index, now: step(index, now, False), carried)
    row_max, row_sum, weighted = step(last, carried, True)
    result = (weighted / row_sum).astype(jnp.bfloat16)
    for h in range(heads):
        out_ref[:, h * HEAD_DIM : (h + 1) * HEAD_DIM] = result[h * TOK_DEV : (h + 1) * TOK_DEV]


def attention(query_rows, kv_all, heads):
    columns, blocks = kv_all.shape[:2]
    parts = max(1, columns * TOK_DEV // 512)
    width = heads * HEAD_DIM
    pairs = blocks * TOK_DEV * heads * columns * blocks * TOK_DEV // 2
    return pl.pallas_call(
        functools.partial(attention_kernel, heads, parts),
        grid=(blocks,),
        out_shape=jax.ShapeDtypeStruct((blocks * TOK_DEV, width), jnp.bfloat16),
        in_specs=[
            pl.BlockSpec((TOK_DEV, width), lambda b: (b, 0)),
            pl.BlockSpec(kv_all.shape, lambda b: (0, 0, 0, 0)),
        ],
        out_specs=pl.BlockSpec((TOK_DEV, width), lambda b: (b, 0)),
        compiler_params=pltpu.CompilerParams(vmem_limit_bytes=56 * 1024 * 1024),
        cost_estimate=pl.CostEstimate(
            flops=pairs * 4 * HEAD_DIM * 4,
            bytes_accessed=kv_all.size * 2,
            transcendentals=pairs,
        ),
        name="attention",
    )(query_rows, kv_all)


def middle_kernel(x_ref, v_ref, down_ref, out_ref, total):
    @pl.when(pl.program_id(0) == 0)
    def _():
        total[...] = jnp.zeros_like(total)

    gate = jnp.dot(x_ref[:, :RANK], v_ref[0, 0], preferred_element_type=jnp.float32)
    up = jnp.dot(x_ref[:, RANK:], v_ref[0, 1], preferred_element_type=jnp.float32)
    hidden = (gate / (1.0 + jnp.exp(-gate)) * up).astype(jnp.bfloat16)
    total[...] += jnp.dot(hidden, down_ref[0], preferred_element_type=jnp.float32)

    @pl.when(pl.program_id(0) == pl.num_programs(0) - 1)
    def _():
        out_ref[...] = total[...]


def middle(rank_in, v_gate_up, u_down):
    rows = rank_in.shape[0]
    units = u_down.shape[1]
    tile = min(1024, units)
    return pl.pallas_call(
        middle_kernel,
        grid=(units // tile,),
        out_shape=jax.ShapeDtypeStruct((rows, RANK), jnp.float32),
        in_specs=[
            pl.BlockSpec((rows, 2 * RANK), lambda i: (0, 0)),
            pl.BlockSpec((1, 2, RANK, tile), lambda i: (0, 0, 0, i)),
            pl.BlockSpec((1, tile, RANK), lambda i: (0, i, 0)),
        ],
        out_specs=pl.BlockSpec((rows, RANK), lambda i: (0, 0)),
        scratch_shapes=[pltpu.VMEM((rows, RANK), jnp.float32)],
        compiler_params=pltpu.CompilerParams(vmem_limit_bytes=48 * 1024 * 1024),
        cost_estimate=pl.CostEstimate(
            flops=rows * RANK * units * 6,
            bytes_accessed=units * RANK * 6,
            transcendentals=rows * units,
        ),
        name="middle",
    )(rank_in, v_gate_up, u_down)


def per_device(
    queries,
    keys,
    values,
    residual,
    proj_weight,
    norm_gain,
    router,
    expert_ids,
    u_gate_up,
    v_gate_up,
    u_down,
    v_down,
):
    seq_count = lax.axis_size("seq")
    exp_count = lax.axis_size("exp")
    heads = HEADS // seq_count
    shares = seq_count // KV_HEADS
    kv_send = jnp.concatenate(
        [keys.reshape(TOK_DEV, KV_HEADS, HEAD_DIM), values.reshape(TOK_DEV, KV_HEADS, HEAD_DIM)],
        axis=-1,
    )
    if shares > 1:
        kv_send = jnp.repeat(kv_send, shares, axis=1)
    kv_send = kv_send.reshape(TOK_DEV, seq_count * 2 * HEAD_DIM)
    kv_got = lax.all_to_all(kv_send, "seq", split_axis=1, concat_axis=0, tiled=True)
    kv_all = lax.all_gather(kv_got, "exp", axis=0, tiled=False)
    query_got = lax.all_to_all(queries, "seq", split_axis=1, concat_axis=0, tiled=True)
    query_got, weight_own = lax.optimization_barrier((query_got, proj_weight))
    weight_rows = lax.all_gather(weight_own, "seq", axis=0, tiled=True)
    kv_all = kv_all.reshape(exp_count, seq_count, TOK_DEV, 2 * HEAD_DIM)
    attended = attention(query_got, kv_all, heads)
    attended = lax.all_to_all(attended, "seq", split_axis=0, concat_axis=1, tiled=True)
    half = TOK_DEV // 2
    first_half, weight_rows = lax.optimization_barrier((attended[:half], weight_rows))
    gathered = [
        lax.all_gather(first_half, "exp", axis=0, tiled=True),
        lax.all_gather(attended[half:], "exp", axis=0, tiled=True),
    ]
    updates = []
    for rows in gathered:
        projected = jnp.dot(rows, weight_rows, preferred_element_type=jnp.float32)
        updates.append(
            lax.all_to_all(
                projected.astype(jnp.bfloat16), "exp", split_axis=0, concat_axis=1, tiled=True
            )
        )
    attn_update = jnp.concatenate(updates, axis=0)
    stream = residual.astype(jnp.float32) + attn_update.astype(jnp.float32)
    mean_sq = jnp.mean(stream * stream, axis=-1, keepdims=True)
    normed = (stream * lax.rsqrt(mean_sq + EPS) * norm_gain.astype(jnp.float32)).astype(
        jnp.bfloat16
    )
    logits = jnp.dot(normed, router, preferred_element_type=jnp.float32)
    expert_range = jnp.arange(EXPERTS, dtype=jnp.int32)
    picked = (expert_ids[:, :, None] == expert_range[None, None, :]).astype(jnp.float32)
    chosen = jnp.sum(picked * logits[:, None, :], axis=-1)
    mix_first = jax.nn.sigmoid(chosen[:, 0] - chosen[:, 1])
    mix_second = jax.nn.sigmoid(chosen[:, 1] - chosen[:, 0])
    piece_count = exp_count // EXPERTS
    piece_width = D // piece_count
    flat_ids = expert_ids.reshape(TOK_DEV * 2)
    member = (flat_ids[:, None] == expert_range[None, :]).astype(jnp.int32)
    slot_of = jnp.sum((jnp.cumsum(member, axis=0) - 1) * member, axis=1)
    dest = (flat_ids * CAP + slot_of).reshape(TOK_DEV, 2)
    places = jnp.arange(EXPERTS * CAP, dtype=jnp.int32)
    first_at = dest[:, 0:1] == places[None, :]
    second_at = dest[:, 1:2] == places[None, :]
    select = (first_at | second_at).astype(jnp.bfloat16)
    send_rows = lax.dot_general(
        select, normed, (((0,), (0,)), ((), ())), preferred_element_type=jnp.float32
    ).astype(jnp.bfloat16)
    if piece_count > 1:
        send_rows = send_rows.reshape(EXPERTS, CAP, piece_count, piece_width).transpose(0, 2, 1, 3)
    send_rows = send_rows.reshape(exp_count, CAP, piece_width)
    dispatched = lax.all_to_all(send_rows, "exp", split_axis=0, concat_axis=0, tiled=True)
    expert_rows = dispatched.reshape(exp_count * CAP, piece_width)
    rank_sum = jnp.dot(expert_rows, u_gate_up[0], preferred_element_type=jnp.float32)
    for bit_index in range(piece_count.bit_length() - 1):
        rank_sum = rank_sum + swapped(rank_sum.astype(jnp.bfloat16), "exp", bit_index).astype(
            rank_sum.dtype
        )
    down_sum = middle(rank_sum.astype(jnp.bfloat16), v_gate_up, u_down)
    for bit_index in range(piece_count.bit_length() - 1):
        down_sum = down_sum + swapped(down_sum.astype(jnp.bfloat16), "exp", bit_index).astype(
            down_sum.dtype
        )
    expert_out = jnp.dot(
        down_sum.astype(jnp.bfloat16), v_down[0], preferred_element_type=jnp.float32
    ).astype(jnp.bfloat16)
    returned = lax.all_to_all(
        expert_out.reshape(exp_count, CAP, piece_width),
        "exp",
        split_axis=0,
        concat_axis=0,
        tiled=True,
    )
    if piece_count > 1:
        returned = returned.reshape(EXPERTS, piece_count, CAP, piece_width).transpose(0, 2, 1, 3)
    returned_rows = returned.reshape(EXPERTS * CAP, D)
    mix = mix_first[:, None] * first_at.astype(jnp.float32) + mix_second[
        :, None
    ] * second_at.astype(jnp.float32)
    mix_high = lax.reduce_precision(mix, 8, 7)
    mix_low = (mix - mix_high).astype(jnp.bfloat16)
    mixture = jnp.dot(
        mix_high.astype(jnp.bfloat16), returned_rows, preferred_element_type=jnp.float32
    ) + jnp.dot(mix_low, returned_rows, preferred_element_type=jnp.float32)
    return (stream + mixture).astype(jnp.bfloat16)


def solution(mesh):
    in_specs = (
        P(("seq", "exp"), None),
        P(("seq", "exp"), None),
        P(("seq", "exp"), None),
        P(("seq", "exp"), None),
        P("seq", "exp"),
        P(),
        P(),
        P(("seq", "exp"), None),
        P("exp", None, None),
        P("exp", None, None, None),
        P("exp", None, None),
        P("exp", None, None),
    )
    out_specs = P(("seq", "exp"), None)
    return jax.shard_map(
        per_device, mesh=mesh, in_specs=in_specs, out_specs=out_specs, check_vma=False
    )
```

profile of v0, /device:TPU:0, one launch (start us, length us, event | category | flops | bytes accessed | tf_op | source)
XLA Modules:
  0.0 475.3 jit_solution(10489104403388478593)
XLA Ops:
  6.5 1.1 copy.79
  7.6 1.0 copy.80
  8.7 0.1 copy.81
  8.8 10.8 %all_to_all.96 = bf16[128,4,256]{2,0,1:T(8,128)(2,1)} all-to-all(bf16[128,4,256]{2,0,1:T(8,128)(2,1)S(1)} %copy.81), channel_id=1, replica_groups=mesh['seq'=4,'exp'=8] {'seq'}, dimensions={1} | all-to-all | bytes 524288 | tf_op jit(solution)/shard_map/all_to_all | solution.py:162
  19.6 0.0 all-gather.5.cloned.1.call-update
  19.7 0.0 all-gather.7.cloned.1.call-start
  19.7 1.2 copy.95
  20.9 13.4 %all_to_all.97 = bf16[128,4,768]{2,0,1:T(8,128)(2,1)} all-to-all(bf16[128,4,768]{2,0,1:T(8,128)(2,1)S(1)} %bitcast.69), channel_id=1, replica_groups=mesh['seq'=4,'exp'=8] {'seq'}, dimensions={1} | all-to-all | bytes 1572864 | tf_op jit(solution)/shard_map/all_to_all | solution.py:164
  34.3 0.0 all-gather.7.cloned.1.call-update
  34.3 0.0 all-gather.11.cloned.1.call-start
  34.4 14.3 %all-gather.5.cloned.1.call-done = bf16[8,512,256]{2,1,0:T(8,128)(2,1)} async-done(((bf16[1,512,256]{2,1,0:T(8,128)(2,1)}), bf16[8,512,256]{2,1,0:T(8,128)(2,1)}) %all-gather.5.cloned.1.call-update) | async-done | bytes 2097168 | tf_op jit(solution)/shard_map/all_gather | solution.py:163
  48.7 16.7 %attention.1 = bf16[512,768]{1,0:T(8,128)(2,1)} custom-call(bf16[512,768]{1,0:T(8,128)(2,1)} %bitcast.74, bf16[8,4,128,256]{3,2,1,0:T(8,128)(2,1)} %bitcast.78), custom_call_target="tpu_custom_call" | custom-call | flops 12884901888 | bytes 2097152 | tf_op jit(solution)/shard_map/attention/pallas_call | solution.py:78
  65.3 16.8 %all_to_all.98 = bf16[4,128,768]{2,1,0:T(8,128)(2,1)S(1)} all-to-all(bf16[4,128,768]{2,1,0:T(8,128)(2,1)} %bitcast.75), channel_id=1, replica_groups=mesh['seq'=4,'exp'=8] {'seq'}, dimensions={0} | all-to-all | bytes 1572864 | tf_op jit(solution)/shard_map/all_to_all | solution.py:169
  82.2 0.1 slice_bitcast_fusion.1
  82.2 0.8 copy.92
  83.0 0.0 all-gather.11.cloned.1.call-update
  83.0 0.0 all-gather.9.cloned.1.call-start
  83.1 0.8 copy.90
  83.8 25.1 %all-gather.7.cloned.1.call-done = bf16[3072,768]{1,0:T(8,128)(2,1)} async-done(((bf16[768,768]{1,0:T(8,128)(2,1)}), bf16[3072,768]{1,0:T(8,128)(2,1)}) %all-gather.7.cloned.1.call-update) | async-done | bytes 4718608 | tf_op jit(solution)/shard_map/all_gather | solution.py:166
  109.0 0.0 all-gather.9.cloned.1.call-update
  109.0 39.9 %all-gather.11.cloned.1.call-done = bf16[512,3072]{1,0:T(8,128)(2,1)} async-done(((bf16[64,3072]{1,0:T(8,128)(2,1)}), bf16[512,3072]{1,0:T(8,128)(2,1)}) %all-gather.11.cloned.1.call-update) | async-done | bytes 3145744 | tf_op jit(solution)/shard_map/all_gather | solution.py:174
  148.9 6.8 %convolution_convert_fusion.2 = bf16[512,768]{1,0:T(8,128)(2,1)} fusion(bf16[512,3072]{1,0:T(8,128)(2,1)} %all-gather.11.cloned.1.call-done, bf16[3072,768]{1,0:T(8,128)(2,1)} %all-gather.7.cloned.1.call-done), kind=kOutput, calls=%fused_computation.12 | convolution fusion | flops 2416312320 | bytes 8650752 | tf_op jit(solution)/shard_map/dot_general | solution.py:178
  155.7 3.5 all-to-all-start.4
  159.2 0.0 copy-start.10
  159.2 0.0 copy-start.9
  159.2 45.2 %all-gather.9.cloned.1.call-done = bf16[512,3072]{1,0:T(8,128)(2,1)} async-done(((bf16[64,3072]{1,0:T(8,128)(2,1)}), bf16[512,3072]{1,0:T(8,128)(2,1)}) %all-gather.9.cloned.1.call-update) | async-done | bytes 3145744 | tf_op jit(solution)/shard_map/all_gather | solution.py:173
  204.4 6.9 %convolution_convert_fusion.3 = bf16[512,768]{1,0:T(8,128)(2,1)} fusion(bf16[512,3072]{1,0:T(8,128)(2,1)} %all-gather.9.cloned.1.call-done, bf16[3072,768]{1,0:T(8,128)(2,1)} %all-gather.7.cloned.1.call-done), kind=kOutput, calls=%fused_computation.13 | convolution fusion | flops 2416312320 | bytes 8650752 | tf_op jit(solution)/shard_map/dot_general | solution.py:178
  211.3 0.0 all-to-all-done.4
  211.3 4.3 all-to-all-start.3
  215.6 0.1 copy.86
  215.8 0.1 eq.72
  215.9 0.1 eq.68
  216.0 0.0 copy-done.9
  216.1 0.6 reduce-window.6
  216.7 0.2 slice_reduce_fusion
  216.9 0.1 fusion.26
  217.0 0.1 reduce_sum.30
  217.2 0.1 copy.88
  217.2 0.1 copy.93
  217.3 0.0 copy-start.5
  217.3 19.3 %all-to-all-done.3 = bf16[8,64,768]{2,1,0:T(8,128)(2,1)} async-done(((bf16[8,64,768]{2,1,0:T(8,128)(2,1)}), bf16[8,64,768]{2,1,0:T(8,128)(2,1)}, u32[]{:S(2)}, u32[]{:S(2)}) %all-to-all-start.3) | async-done | bytes 786464 | tf_op jit(solution)/shard_map/all_to_all | solution.py:180
  236.6 1.2 copy.91
  237.8 0.6 multiply_reduce_fusion
  238.4 0.6 multiply_convert_fusion
  239.0 0.0 copy-start.3
  239.1 1.1 copy-done.3
  240.2 1.1 convolution_convert_fusion.1
  241.3 3.0 reshape.78
  244.3 92.8 %all_to_all.99 = bf16[8,33,6144]{2,1,0:T(8,128)(2,1)} all-to-all(bf16[8,33,6144]{2,1,0:T(8,128)(2,1)} %reshape.78), channel_id=1, replica_groups=mesh['seq'=4,'exp'=8] {'exp'}, dimensions={0} | all-to-all | bytes 6488064 | tf_op jit(solution)/shard_map/all_to_all | solution.py:212
  337.2 3.3 reshape.79
  340.4 6.6 %fusion.5.x_ref = bf16[264,1024]{1,0:T(8,128)(2,1)S(1)} fusion(bf16[264,6144]{1,0:T(8,128)(2,1)S(1)} %reshape.79, bf16[1,6144,1024]{2,1,0:T(8,128)(2,1)} %param.20), kind=kOutput, calls=%fused_computation.14 | convolution fusion | flops 3322159104 | bytes 16367616 | tf_op jit(solution)/shard_map/dot_general | solution.py:214
  347.0 13.4 %middle.1 = f32[264,512]{1,0:T(8,128)S(1)} custom-call(bf16[264,1024]{1,0:T(8,128)(2,1)S(1)} %fusion.5.x_ref, bf16[1,2,512,8192]{3,2,1,0:T(8,128)(2,1)} %v_ref.1, bf16[1,8192,512]{2,1,0:T(8,128)(2,1)} %down_ref.1), custom_call_target="tpu_custom_call" | custom-call | flops 6643777536 | bytes 25165824 | tf_op jit(solution)/shard_map/middle/pallas_call | solution.py:116
  360.4 4.6 convolution_convert_fusion
  365.1 3.1 reshape.80
  368.1 4.7 all-to-all-start.6
  372.8 0.5 fusion.30
  373.4 87.8 %all-to-all-done.6 = bf16[8,33,6144]{2,1,0:T(8,128)(2,1)} async-done(((bf16[8,33,6144]{2,1,0:T(8,128)(2,1)}), bf16[8,33,6144]{2,1,0:T(8,128)(2,1)}, u32[]{:S(2)}, u32[]{:S(2)}) %all-to-all-start.6) | async-done | bytes 3244064 | tf_op jit(solution)/shard_map/all_to_all | solution.py:227
  461.2 3.3 reshape.81
  464.4 0.0 copy-start.2
  464.5 1.1 fusion.13
  465.6 0.3 copy-done.2
  465.9 0.2 copy-done.6
  466.1 0.2 copy-done.8
  466.3 2.5 fusion.3
  (23 shorter events, 0.2 us)
Async XLA Ops:
  6.5 366.3 %copy-start = (bf16[6144,8]{0,1:T(8,128)(2,1)S(1)}, bf16[6144,8]{0,1:T(8,128)(2,1)}, u32[]{:S(2)}) copy-start(bf16[6144,8]{0,1:T(8,128)(2,1)} %param.18) | copy-start | bytes 294916
  6.5 42.1 %all-gather.5.cloned.1.call-start = ((), (), s32[]{:S(2)}) async-start(), calls=%async_computation.7 | async-start | bytes 2359296 | tf_op jit(solution)/shard_map/all_gather | solution.py:163
  19.7 89.3 %all-gather.7.cloned.1.call-start = ((), (), s32[]{:S(2)}) async-start(), calls=%async_computation.8 | async-start | bytes 5898240 | tf_op jit(solution)/shard_map/all_gather | solution.py:166
  34.3 114.6 %all-gather.11.cloned.1.call-start = ((), (), s32[]{:S(2)}) async-start(), calls=%async_computation.10 | async-start | bytes 3538944 | tf_op jit(solution)/shard_map/all_gather | solution.py:174
  83.0 121.4 %all-gather.9.cloned.1.call-start = ((), (), s32[]{:S(2)}) async-start(), calls=%async_computation.9 | async-start | bytes 3538944 | tf_op jit(solution)/shard_map/all_gather | solution.py:173
  155.7 55.6 %all-to-all-start.4 = ((bf16[8,64,768]{2,1,0:T(8,128)(2,1)}), bf16[8,64,768]{2,1,0:T(8,128)(2,1)S(1)}, u32[]{:S(2)}, u32[]{:S(2)}) async-start(bf16[8,64,768]{2,1,0:T(8,128)(2,1)} %bitcast.11), calls=%async_computation.4 | async-start | bytes 1572864 | tf_op jit(solution)/shard_map/all_to_all | solution.py:180
  159.2 56.4 %copy-start.10 = (s32[128,2]{0,1:T(2,128)S(1)}, s32[128,2]{0,1:T(2,128)}, u32[]{:S(2)}) copy-start(s32[128,2]{0,1:T(2,128)} %param.19) | copy-start | bytes 3076
  159.2 56.8 %copy-start.9 = (bf16[6144]{0:T(1024)(128)(2,1)S(1)}, bf16[6144]{0:T(1024)(128)(2,1)}, u32[]{:S(2)}) copy-start(bf16[6144]{0:T(1024)(128)(2,1)} %param.17) | copy-start | bytes 36868
  211.3 26.5 %copy-start.1 = (bf16[128,6144]{1,0:T(8,128)(2,1)S(1)}, bf16[128,6144]{1,0:T(8,128)(2,1)}, u32[]{:S(2)}) copy-start(bf16[128,6144]{1,0:T(8,128)(2,1)} %param.15) | copy-start | bytes 4718596
  211.3 25.3 %all-to-all-start.3 = ((bf16[8,64,768]{2,1,0:T(8,128)(2,1)}), bf16[8,64,768]{2,1,0:T(8,128)(2,1)}, u32[]{:S(2)}, u32[]{:S(2)}) async-start(bf16[8,64,768]{2,1,0:T(8,128)(2,1)} %bitcast.9), calls=%async_computation.3 | async-start | bytes 1572864 | tf_op jit(solution)/shard_map/all_to_all | solution.py:180
  217.3 21.7 %copy-start.5 = (bf16[8,8,8,768]{3,2,0,1:T(8,128)(2,1)}, bf16[8,8,8,768]{3,2,0,1:T(8,128)(2,1)S(1)}, u32[]{:S(2)}) copy-start(bf16[8,8,8,768]{3,2,0,1:T(8,128)(2,1)S(1)} %copy.93) | copy-start | bytes 2359300
  237.8 1.3 copy-start.7
  239.0 1.1 copy-start.3
  368.1 4.7 copy-start.4
  368.1 93.0 %all-to-all-start.6 = ((bf16[8,33,6144]{2,1,0:T(8,128)(2,1)}), bf16[8,33,6144]{2,1,0:T(8,128)(2,1)}, u32[]{:S(2)}, u32[]{:S(2)}) async-start(bf16[8,33,6144]{2,1,0:T(8,128)(2,1)} %reshape.80), calls=%async_computation.6 | async-start | bytes 7864320 | tf_op jit(solution)/shard_map/all_to_all | solution.py:227
  464.4 1.4 copy-start.2
  464.5 1.6 copy-start.6
  464.5 1.8 copy-start.8
Sparse Core Ops, SparseCore 0:
  19.8 28.8 all-gather.4
  50.5 58.4 all-gather.6
  110.6 38.2 all-gather.10
  150.4 53.9 all-gather.8
where the time goes:
time: 476 us; the launch traced here: 475 us
  waiting for transfers between devices  232 us (49%)
  blocking collectives  134 us (28%)
  Pallas kernels  30.1 us (6%)
  matrix products  30 us (6%)
  local copies, waits for them, and re-layouts  21.6 us (5%)
  between operations  13.5 us (3%)
  starting transfers between devices  12.7 us (3%)
    all_to_all x1, blocking collectives, per_device(): lax.all_to_all(send_rows, 'exp', split_axis=0, concat_axis=0, tiled=True)  92.8 us
    all_to_all x1, waiting for transfers between devices, per_device(): lax.all_to_all(expert_out.reshape(exp_count, CAP, piece_width), 'exp', sp...  87.8 us
    all_gather x1, waiting for transfers between devices, per_device(): lax.all_gather(first_half, 'exp', axis=0, tiled=True)  45.2 us
    all_gather x1, waiting for transfers between devices, per_device(): lax.all_gather(attended[half:], 'exp', axis=0, tiled=True)  39.9 us
    all_gather x1, waiting for transfers between devices, per_device(): weight_rows = lax.all_gather(weight_own, 'seq', axis=0, tiled=True)  25.1 us
    all_to_all x2, waiting for transfers between devices, per_device(): lax.all_to_all(projected.astype(jnp.bfloat16), 'exp', split_axis=0, conca...  19.3 us
    all_to_all x1, blocking collectives, per_device(): lax.all_to_all(attended, 'seq', split_axis=0, concat_axis=1, tiled=True)  16.8 us
    pallas_call x1, Pallas kernels, attention(): pl.pallas_call(functools.partial(attention_kernel, heads, parts), grid=(b...  16.7 us
  transfers between devices with their start and end apart: 7, of which 6 were waited for; matrix products, arithmetic and copies ran while one was open for 4% of the time, Pallas kernels for 4%

commit v1 on v0

--- a/solution.py
+++ b/solution.py
@@ -19,10 +19,6 @@
 
 EPS = 1e-05
 LOG2_E = 1.4426950408889634
-
-
-def swapped(x, axis, distance):
-    return lax.ppermute(x, axis, [(i, i ^ 1 << distance) for i in range(lax.axis_size(axis))])
 
 
 def attention_kernel(heads, parts, q_ref, kv_ref, out_ref):
@@ -94,44 +90,324 @@
     )(query_rows, kv_all)
 
 
-def middle_kernel(x_ref, v_ref, down_ref, out_ref, total):
-    @pl.when(pl.program_id(0) == 0)
-    def _():
-        total[...] = jnp.zeros_like(total)
-
-    gate = jnp.dot(x_ref[:, :RANK], v_ref[0, 0], preferred_element_type=jnp.float32)
-    up = jnp.dot(x_ref[:, RANK:], v_ref[0, 1], preferred_element_type=jnp.float32)
-    hidden = (gate / (1.0 + jnp.exp(-gate)) * up).astype(jnp.bfloat16)
-    total[...] += jnp.dot(hidden, down_ref[0], preferred_element_type=jnp.float32)
-
-    @pl.when(pl.program_id(0) == pl.num_programs(0) - 1)
-    def _():
-        out_ref[...] = total[...]
-
-
-def middle(rank_in, v_gate_up, u_down):
-    rows = rank_in.shape[0]
+MAIN = CAP // 16 * 16
+PAD = 16
+
+
+def flipped(index, bits):
+    bit = 1
+    while bit <= bits:
+        if bits & bit:
+            index = index + bit * (1 - 2 * ((index // bit) % 2))
+        bit *= 2
+    return index
+
+
+def to_exp(peer):
+    return {"device_id": {"exp": peer}, "device_id_type": pl.DeviceIdType.MESH}
+
+
+def gather_lanes(ref, chunk, tiles):
+    return jnp.concatenate([ref[chunk, :, t, :] for t in range(tiles)], axis=1)
+
+
+def padded(rows):
+    count = rows.shape[0]
+    if count % PAD:
+        rows = jnp.concatenate(
+            [rows, jnp.zeros((PAD - count % PAD, rows.shape[1]), rows.dtype)], axis=0
+        )
+    return rows.astype(jnp.bfloat16)
+
+
+def experts_kernel(
+    count,
+    pieces,
+    chunks,
+    steps,
+    x_ref,
+    sel_ref,
+    mix_ref,
+    stream_ref,
+    u_hbm,
+    vg_hbm,
+    ud_hbm,
+    vd_hbm,
+    out_ref,
+    u_buf,
+    vg_buf,
+    ud_buf,
+    vd_buf,
+    send,
+    recv,
+    back,
+    send_x,
+    recv_x,
+    back_x,
+    rank_sum,
+    rank_in,
+    swap,
+    w_sem,
+    send_sem,
+    recv_sem,
+    send_x_sem,
+    recv_x_sem,
+    swap_sem,
+):
+    me = lax.axis_index("exp")
+    experts = count // pieces
+    width = send.shape[-1]
+    tiles = width // 128
+    unit = vg_buf.shape[-1]
+    barrier = pltpu.get_barrier_semaphore()
+    for d in range(1, count):
+        pl.semaphore_signal(barrier, inc=1, **to_exp(flipped(me, d)))
+
+    def u_copy(c):
+        rows = pl.ds(pl.multiple_of(c * width, width), width)
+        return pltpu.make_async_copy(u_hbm.at[0, rows], u_buf.at[c], w_sem.at[0, c])
+
+    def vg_copy(f):
+        cols = pl.ds(pl.multiple_of(f * unit, unit), unit)
+        return pltpu.make_async_copy(vg_hbm.at[0, :, :, cols], vg_buf.at[f], w_sem.at[1, f])
+
+    def ud_copy(f):
+        rows = pl.ds(pl.multiple_of(f * unit, unit), unit)
+        return pltpu.make_async_copy(ud_hbm.at[0, rows], ud_buf.at[f], w_sem.at[2, f])
+
+    def vd_copy(c):
+        cols = pl.ds(pl.multiple_of(c * width, width), width)
+        return pltpu.make_async_copy(vd_hbm.at[0, :, cols], vd_buf.at[c], w_sem.at[3, c])
+
+    for c in range(chunks):
+        u_copy(c).start()
+    for f in range(steps):
+        vg_copy(f).start()
+        ud_copy(f).start()
+    for c in range(chunks):
+        vd_copy(c).start()
+
+    def fill(c, piece, rows):
+        for k in range(experts):
+            send[c, k * pieces + piece] = rows[k * MAIN : (k + 1) * MAIN].astype(jnp.bfloat16)
+        extra = rows[experts * MAIN : experts * MAIN + experts]
+        for t in range(tiles):
+            lanes = extra[:, t * 128 : (t + 1) * 128]
+            if pieces == 1:
+                send_x[c, :, t, :] = lanes
+            else:
+                for k in range(experts):
+                    send_x[c, k * pieces + piece, t : t + 1, :] = lanes[k : k + 1]
+
+    def copies(phase, c, peer, into, into_x):
+        main = pltpu.make_async_remote_copy(
+            src_ref=send.at[c, peer],
+            dst_ref=into.at[c, me],
+            send_sem=send_sem.at[phase, c, peer],
+            recv_sem=recv_sem.at[phase, c, me],
+            **to_exp(peer),
+        )
+        extra = pltpu.make_async_remote_copy(
+            src_ref=send_x.at[c, peer],
+            dst_ref=into_x.at[c, me],
+            send_sem=send_x_sem.at[phase, c, peer],
+            recv_sem=recv_x_sem.at[phase, c, me],
+            **to_exp(peer),
+        )
+        return main, extra
+
+    def arrivals(phase, c, peer, into, into_x):
+        main = pltpu.make_async_remote_copy(
+            src_ref=send.at[c, peer],
+            dst_ref=into.at[c, peer],
+            send_sem=send_sem.at[phase, c, peer],
+            recv_sem=recv_sem.at[phase, c, peer],
+            **to_exp(peer),
+        )
+        extra = pltpu.make_async_remote_copy(
+            src_ref=send_x.at[c, peer],
+            dst_ref=into_x.at[c, peer],
+            send_sem=send_x_sem.at[phase, c, peer],
+            recv_sem=recv_x_sem.at[phase, c, peer],
+            **to_exp(peer),
+        )
+        return main, extra
+
+    def send_all(phase, c, into, into_x):
+        for d in range(1, count):
+            for copy in copies(phase, c, flipped(me, d), into, into_x):
+                copy.start()
+        into[c, me] = send[c, me]
+        into_x[c, me] = send_x[c, me]
+
+    def wait_sent(phase, c, into, into_x):
+        for d in range(1, count):
+            for copy in arrivals(phase, c, flipped(me, d), into, into_x):
+                copy.wait_send()
+
+    def wait_got(phase, c, into, into_x):
+        for d in range(1, count):
+            for copy in arrivals(phase, c, flipped(me, d), into, into_x):
+                copy.wait_recv()
+
+    def fill_first(c):
+        for piece in range(pieces):
+            start = pl.multiple_of(piece * chunks * width + c * width, width)
+            fill(
+                c,
+                piece,
+                jnp.dot(
+                    sel_ref[...],
+                    x_ref[:, pl.ds(start, width)],
+                    preferred_element_type=jnp.float32,
+                ),
+            )
+
+    fill_first(0)
+    pl.semaphore_wait(barrier, count - 1)
+    send_all(0, 0, recv, recv_x)
+
+    def dispatch(c, carried):
+        fill_first(c)
+        send_all(0, c, recv, recv_x)
+        return carried
+
+    lax.fori_loop(1, chunks, dispatch, 0)
+    rank_sum[...] = jnp.zeros_like(rank_sum)
+
+    def first_factor(c, carried):
+        u_copy(c).wait()
+        wait_got(0, c, recv, recv_x)
+        rows = jnp.concatenate(
+            [recv[c].reshape(count * MAIN, width), padded(gather_lanes(recv_x, c, tiles))], axis=0
+        )
+        rank_sum[...] += jnp.dot(rows, u_buf[c], preferred_element_type=jnp.float32)
+        return carried
+
+    lax.fori_loop(0, chunks, first_factor, 0)
+
+    def add_pieces(slot, columns):
+        bit = 1
+        while bit < pieces:
+            swap[slot, 0, :, :columns] = rank_sum[:, :columns].astype(jnp.bfloat16)
+            copy = pltpu.make_async_remote_copy(
+                src_ref=swap.at[slot, 0],
+                dst_ref=swap.at[slot, 1],
+                send_sem=swap_sem.at[slot, 0],
+                recv_sem=swap_sem.at[slot, 1],
+                **to_exp(flipped(me, bit)),
+            )
+            copy.start()
+            copy.wait()
+            rank_sum[:, :columns] += swap[slot, 1, :, :columns].astype(jnp.float32)
+            bit *= 2
+            slot += 1
+        return slot
+
+    slot = add_pieces(0, 2 * RANK)
+    rank_in[...] = rank_sum[...].astype(jnp.bfloat16)
+    rank_sum[:, :RANK] = jnp.zeros((rank_sum.shape[0], RANK), jnp.float32)
+
+    def middle(f, carried):
+        vg_copy(f).wait()
+        ud_copy(f).wait()
+        gate = jnp.dot(rank_in[:, :RANK], vg_buf[f, 0], preferred_element_type=jnp.float32)
+        up = jnp.dot(rank_in[:, RANK:], vg_buf[f, 1], preferred_element_type=jnp.float32)
+        hidden = (gate / (1.0 + jnp.exp(-gate)) * up).astype(jnp.bfloat16)
+        rank_sum[:, :RANK] += jnp.dot(hidden, ud_buf[f], preferred_element_type=jnp.float32)
+        return carried
+
+    lax.fori_loop(0, steps, middle, 0)
+    add_pieces(slot, RANK)
+    rank_in[:, :RANK] = rank_sum[:, :RANK].astype(jnp.bfloat16)
+
+    def last_factor(c, carried):
+        vd_copy(c).wait()
+        wait_sent(0, c, recv, recv_x)
+        rows = jnp.dot(rank_in[:, :RANK], vd_buf[c], preferred_element_type=jnp.float32)
+        for k in range(count):
+            send[c, k] = rows[k * MAIN : (k + 1) * MAIN].astype(jnp.bfloat16)
+        extra = rows[count * MAIN : count * MAIN + count]
+        for t in range(tiles):
+            send_x[c, :, t, :] = extra[:, t * 128 : (t + 1) * 128]
+        send_all(1, c, back, back_x)
+        return carried
+
+    lax.fori_loop(0, chunks, last_factor, 0)
+
+    def combine(c, carried):
+        wait_got(1, c, back, back_x)
+        for piece in range(pieces):
+            rows = back[c].reshape(experts, pieces, MAIN, width)[:, piece]
+            extra = gather_lanes(back_x, c, tiles).reshape(experts, pieces, width)[:, piece]
+            rows = jnp.concatenate([rows.reshape(experts * MAIN, width), padded(extra)], axis=0)
+            both = jnp.dot(mix_ref[...], rows, preferred_element_type=jnp.float32)
+            start = pl.multiple_of(piece * chunks * width + c * width, width)
+            cols = pl.ds(start, width)
+            out_ref[:, cols] = (
+                stream_ref[:, cols] + both[:TOK_DEV] + both[TOK_DEV:]
+            ).astype(jnp.bfloat16)
+        return carried
+
+    lax.fori_loop(0, chunks, combine, 0)
+
+    def drain(c, carried):
+        wait_sent(1, c, back, back_x)
+        return carried
+
+    lax.fori_loop(0, chunks, drain, 0)
+
+
+def experts_layer(normed, select, mix, stream, u_gate_up, v_gate_up, u_down, v_down, chunks):
+    count = lax.axis_size("exp")
+    pieces = count // EXPERTS
+    width = D // pieces // chunks
     units = u_down.shape[1]
-    tile = min(1024, units)
+    unit = min(1024, units)
+    steps = units // unit
+    rows = count * MAIN + PAD * (-(-count // PAD))
+    swaps = max(1, 2 * (pieces.bit_length() - 1))
+    vmem = pl.BlockSpec(memory_space=pltpu.VMEM)
+    anywhere = pl.BlockSpec(memory_space=pl.ANY)
+    dma = pltpu.SemaphoreType.DMA
+    block = (chunks, count, MAIN, width)
+    block_x = (chunks, count, width // 128, 128)
     return pl.pallas_call(
-        middle_kernel,
-        grid=(units // tile,),
-        out_shape=jax.ShapeDtypeStruct((rows, RANK), jnp.float32),
-        in_specs=[
-            pl.BlockSpec((rows, 2 * RANK), lambda i: (0, 0)),
-            pl.BlockSpec((1, 2, RANK, tile), lambda i: (0, 0, 0, i)),
-            pl.BlockSpec((1, tile, RANK), lambda i: (0, i, 0)),
+        functools.partial(experts_kernel, count, pieces, chunks, steps),
+        out_shape=jax.ShapeDtypeStruct((TOK_DEV, D), jnp.bfloat16),
+        in_specs=[vmem] * 4 + [anywhere] * 4,
+        out_specs=vmem,
+        scratch_shapes=[
+            pltpu.VMEM((chunks, width, 2 * RANK), jnp.bfloat16),
+            pltpu.VMEM((steps, 2, RANK, unit), jnp.bfloat16),
+            pltpu.VMEM((steps, unit, RANK), jnp.bfloat16),
+            pltpu.VMEM((chunks, RANK, width), jnp.bfloat16),
+            pltpu.VMEM(block, jnp.bfloat16),
+            pltpu.VMEM(block, jnp.bfloat16),
+            pltpu.VMEM(block, jnp.bfloat16),
+            pltpu.VMEM(block_x, jnp.float32),
+            pltpu.VMEM(block_x, jnp.float32),
+            pltpu.VMEM(block_x, jnp.float32),
+            pltpu.VMEM((rows, 2 * RANK), jnp.float32),
+            pltpu.VMEM((rows, 2 * RANK), jnp.bfloat16),
+            pltpu.VMEM((swaps, 2, rows, 2 * RANK) if pieces > 1 else (1, 2, 16, 128), jnp.bfloat16),
+            dma((4, max(chunks, steps))),
+            dma((2, chunks, count)),
+            dma((2, chunks, count)),
+            dma((2, chunks, count)),
+            dma((2, chunks, count)),
+            dma((swaps, 2)),
         ],
-        out_specs=pl.BlockSpec((rows, RANK), lambda i: (0, 0)),
-        scratch_shapes=[pltpu.VMEM((rows, RANK), jnp.float32)],
-        compiler_params=pltpu.CompilerParams(vmem_limit_bytes=48 * 1024 * 1024),
+        compiler_params=pltpu.CompilerParams(
+            collective_id=0, has_side_effects=True, vmem_limit_bytes=67043328
+        ),
         cost_estimate=pl.CostEstimate(
             flops=rows * RANK * units * 6,
             bytes_accessed=units * RANK * 6,
             transcendentals=rows * units,
         ),
-        name="middle",
-    )(rank_in, v_gate_up, u_down)
+        name="experts",
+    )(normed, select, mix, stream, u_gate_up, v_gate_up, u_down, v_down)
 
 
 def per_device(
@@ -193,56 +469,27 @@
     chosen = jnp.sum(picked * logits[:, None, :], axis=-1)
     mix_first = jax.nn.sigmoid(chosen[:, 0] - chosen[:, 1])
     mix_second = jax.nn.sigmoid(chosen[:, 1] - chosen[:, 0])
-    piece_count = exp_count // EXPERTS
-    piece_width = D // piece_count
     flat_ids = expert_ids.reshape(TOK_DEV * 2)
     member = (flat_ids[:, None] == expert_range[None, :]).astype(jnp.int32)
     slot_of = jnp.sum((jnp.cumsum(member, axis=0) - 1) * member, axis=1)
-    dest = (flat_ids * CAP + slot_of).reshape(TOK_DEV, 2)
-    places = jnp.arange(EXPERTS * CAP, dtype=jnp.int32)
+    dest = jnp.where(
+        slot_of < MAIN, flat_ids * MAIN + slot_of, EXPERTS * MAIN + flat_ids + (slot_of - MAIN)
+    ).reshape(TOK_DEV, 2)
+    places = jnp.arange(EXPERTS * MAIN + PAD, dtype=jnp.int32)
     first_at = dest[:, 0:1] == places[None, :]
     second_at = dest[:, 1:2] == places[None, :]
-    select = (first_at | second_at).astype(jnp.bfloat16)
-    send_rows = lax.dot_general(
-        select, normed, (((0,), (0,)), ((), ())), preferred_element_type=jnp.float32
+    select = (
+        (dest[:, 0][None, :] == places[:, None]) | (dest[:, 1][None, :] == places[:, None])
     ).astype(jnp.bfloat16)
-    if piece_count > 1:
-        send_rows = send_rows.reshape(EXPERTS, CAP, piece_count, piece_width).transpose(0, 2, 1, 3)
-    send_rows = send_rows.reshape(exp_count, CAP, piece_width)
-    dispatched = lax.all_to_all(send_rows, "exp", split_axis=0, concat_axis=0, tiled=True)
-    expert_rows = dispatched.reshape(exp_count * CAP, piece_width)
-    rank_sum = jnp.dot(expert_rows, u_gate_up[0], preferred_element_type=jnp.float32)
-    for bit_index in range(piece_count.bit_length() - 1):
-        rank_sum = rank_sum + swapped(rank_sum.astype(jnp.bfloat16), "exp", bit_index).astype(
-            rank_sum.dtype
-        )
-    down_sum = middle(rank_sum.astype(jnp.bfloat16), v_gate_up, u_down)
-    for bit_index in range(piece_count.bit_length() - 1):
-        down_sum = down_sum + swapped(down_sum.astype(jnp.bfloat16), "exp", bit_index).astype(
-            down_sum.dtype
-        )
-    expert_out = jnp.dot(
-        down_sum.astype(jnp.bfloat16), v_down[0], preferred_element_type=jnp.float32
-    ).astype(jnp.bfloat16)
-    returned = lax.all_to_all(
-        expert_out.reshape(exp_count, CAP, piece_width),
-        "exp",
-        split_axis=0,
-        concat_axis=0,
-        tiled=True,
-    )
-    if piece_count > 1:
-        returned = returned.reshape(EXPERTS, piece_count, CAP, piece_width).transpose(0, 2, 1, 3)
-    returned_rows = returned.reshape(EXPERTS * CAP, D)
     mix = mix_first[:, None] * first_at.astype(jnp.float32) + mix_second[
         :, None
     ] * second_at.astype(jnp.float32)
     mix_high = lax.reduce_precision(mix, 8, 7)
     mix_low = (mix - mix_high).astype(jnp.bfloat16)
-    mixture = jnp.dot(
-        mix_high.astype(jnp.bfloat16), returned_rows, preferred_element_type=jnp.float32
-    ) + jnp.dot(mix_low, returned_rows, preferred_element_type=jnp.float32)
-    return (stream + mixture).astype(jnp.bfloat16)
+    mix_both = jnp.concatenate([mix_high.astype(jnp.bfloat16), mix_low], axis=0)
+    return experts_layer(
+        normed, select, mix_both, stream, u_gate_up, v_gate_up, u_down, v_down, 3
+    )
 
 
 def solution(mesh):

time: 476 us -> 416 us (0.87)
  Pallas kernels: 30.1 us -> 176 us
  blocking collectives: 134 us -> 41 us
  waiting for transfers between devices: 232 us -> 143 us
  matrix products: 30 us -> 14.1 us
  local copies, waits for them, and re-layouts: 21.6 us -> 10.9 us
    pallas_call x1, Pallas kernels: 13.4 us -> 160 us  [experts_layer(): pl.pallas_call(functools.partial(experts_kernel, count, pieces, chunks, s...]
    all_to_all x1 -> x0, blocking collectives: 92.8 us -> none  [per_device(): lax.all_to_all(send_rows, 'exp', split_axis=0, concat_axis=0, tiled=True)]
    all_to_all x1 -> x0, waiting for transfers between devices: 87.8 us -> none  [per_device(): lax.all_to_all(expert_out.reshape(exp_count, CAP, piece_width), 'exp', sp...]
    dot_general x5 -> x0, matrix products: 15.9 us -> none  [the longest x1 6.56 us: per_device(): jnp.dot(expert_rows, u_gate_up[0], preferred_element_type=jnp.float32)]
    reshape x4 -> x0, local copies, waits for them, and re-layouts: 12.7 us -> none  [the longest x1 3.28 us: per_device(): expert_rows = dispatched.reshape(exp_count * CAP, piece_width)]
  transfers between devices with their start and end apart: 7 -> 6, of which waited for: 6 -> 5; matrix products, arithmetic and copies ran while one was open for 4% -> 5% of each run, Pallas kernels for 4% -> 4%
where the time goes in v1:
time: 416 us; the launch traced here: 412 us
  Pallas kernels  176 us (42%)
  waiting for transfers between devices  143 us (34%)
  blocking collectives  41 us (10%)
  matrix products  14.1 us (3%)
  between operations  13.3 us (3%)
  local copies, waits for them, and re-layouts  10.9 us (3%)
  starting transfers between devices  8.2 us (2%)
  other arithmetic  5.1 us (1%)
    pallas_call x1, Pallas kernels, experts_layer(): pl.pallas_call(functools.partial(experts_kernel, count, pieces, chunks, s...  160 us
    all_gather x1, waiting for transfers between devices, per_device(): lax.all_gather(first_half, 'exp', axis=0, tiled=True)  45.2 us
    all_gather x1, waiting for transfers between devices, per_device(): lax.all_gather(attended[half:], 'exp', axis=0, tiled=True)  39.9 us
    all_gather x1, waiting for transfers between devices, per_device(): weight_rows = lax.all_gather(weight_own, 'seq', axis=0, tiled=True)  25.1 us
    all_to_all x2, waiting for transfers between devices, per_device(): lax.all_to_all(projected.astype(jnp.bfloat16), 'exp', split_axis=0, conca...  18.4 us
    all_to_all x1, blocking collectives, per_device(): lax.all_to_all(attended, 'seq', split_axis=0, concat_axis=1, tiled=True)  16.8 us
    pallas_call x1, Pallas kernels, attention(): pl.pallas_call(functools.partial(attention_kernel, heads, parts), grid=(b...  16.7 us
    all_gather x1, waiting for transfers between devices, per_device(): kv_all = lax.all_gather(kv_got, 'exp', axis=0, tiled=False)  14.3 us
  transfers between devices with their start and end apart: 6, of which 5 were waited for; matrix products, arithmetic and copies ran while one was open for 5% of the time, Pallas kernels for 4%

profile of v1, /device:TPU:0, one launch (start us, length us, event | category | flops | bytes accessed | tf_op | source)
XLA Modules:
  0.0 412.0 jit_solution(9861346730606143592)
XLA Ops:
  6.5 0.0 all-gather.5.cloned.1.call-start
  6.5 1.0 copy.89
  7.6 1.0 copy.90
  8.6 0.1 copy.91
  8.8 10.8 %all_to_all.86 = bf16[128,4,256]{2,0,1:T(8,128)(2,1)} all-to-all(bf16[128,4,256]{2,0,1:T(8,128)(2,1)S(1)} %copy.91), channel_id=1, replica_groups=mesh['seq'=4,'exp'=8] {'seq'}, dimensions={1} | all-to-all | bytes 524288 | tf_op jit(solution)/shard_map/all_to_all | solution.py:438
  19.6 0.0 all-gather.5.cloned.1.call-update
  19.6 0.0 all-gather.7.cloned.1.call-start
  19.7 1.2 copy.107
  20.9 13.4 %all_to_all.87 = bf16[128,4,768]{2,0,1:T(8,128)(2,1)} all-to-all(bf16[128,4,768]{2,0,1:T(8,128)(2,1)S(1)} %bitcast.55), channel_id=1, replica_groups=mesh['seq'=4,'exp'=8] {'seq'}, dimensions={1} | all-to-all | bytes 1572864 | tf_op jit(solution)/shard_map/all_to_all | solution.py:440
  34.3 0.0 all-gather.7.cloned.1.call-update
  34.3 0.0 all-gather.11.cloned.1.call-start
  34.3 14.3 %all-gather.5.cloned.1.call-done = bf16[8,512,256]{2,1,0:T(8,128)(2,1)} async-done(((bf16[1,512,256]{2,1,0:T(8,128)(2,1)}), bf16[8,512,256]{2,1,0:T(8,128)(2,1)}) %all-gather.5.cloned.1.call-update) | async-done | bytes 2097168 | tf_op jit(solution)/shard_map/all_gather | solution.py:439
  48.6 16.7 %attention.1 = bf16[512,768]{1,0:T(8,128)(2,1)} custom-call(bf16[512,768]{1,0:T(8,128)(2,1)} %bitcast.60, bf16[8,4,128,256]{3,2,1,0:T(8,128)(2,1)} %bitcast.64), custom_call_target="tpu_custom_call" | custom-call | flops 12884901888 | bytes 2097152 | tf_op jit(solution)/shard_map/attention/pallas_call | solution.py:74
  65.3 16.8 %all_to_all.88 = bf16[4,128,768]{2,1,0:T(8,128)(2,1)S(1)} all-to-all(bf16[4,128,768]{2,1,0:T(8,128)(2,1)} %bitcast.61), channel_id=1, replica_groups=mesh['seq'=4,'exp'=8] {'seq'}, dimensions={0} | all-to-all | bytes 1572864 | tf_op jit(solution)/shard_map/all_to_all | solution.py:445
  82.1 0.1 slice_bitcast_fusion.1
  82.2 0.8 copy.104
  83.0 0.0 all-gather.11.cloned.1.call-update
  83.0 0.0 all-gather.9.cloned.1.call-start
  83.0 0.8 copy.102
  83.8 25.1 %all-gather.7.cloned.1.call-done = bf16[3072,768]{1,0:T(8,128)(2,1)} async-done(((bf16[768,768]{1,0:T(8,128)(2,1)}), bf16[3072,768]{1,0:T(8,128)(2,1)}) %all-gather.7.cloned.1.call-update) | async-done | bytes 4718608 | tf_op jit(solution)/shard_map/all_gather | solution.py:442
  109.0 0.0 all-gather.9.cloned.1.call-update
  109.0 39.9 %all-gather.11.cloned.1.call-done = bf16[512,3072]{1,0:T(8,128)(2,1)} async-done(((bf16[64,3072]{1,0:T(8,128)(2,1)}), bf16[512,3072]{1,0:T(8,128)(2,1)}) %all-gather.11.cloned.1.call-update) | async-done | bytes 3145744 | tf_op jit(solution)/shard_map/all_gather | solution.py:450
  148.9 6.8 %convolution_convert_fusion = bf16[512,768]{1,0:T(8,128)(2,1)} fusion(bf16[512,3072]{1,0:T(8,128)(2,1)} %all-gather.11.cloned.1.call-done, bf16[3072,768]{1,0:T(8,128)(2,1)} %all-gather.7.cloned.1.call-done), kind=kOutput, calls=%fused_computation.3 | convolution fusion | flops 2416312320 | bytes 8650752 | tf_op jit(solution)/shard_map/dot_general | solution.py:454
  155.6 3.5 all-to-all-start.4
  159.2 0.0 copy-start.4
  159.2 0.0 copy-start.3
  159.2 45.2 %all-gather.9.cloned.1.call-done = bf16[512,3072]{1,0:T(8,128)(2,1)} async-done(((bf16[64,3072]{1,0:T(8,128)(2,1)}), bf16[512,3072]{1,0:T(8,128)(2,1)}) %all-gather.9.cloned.1.call-update) | async-done | bytes 3145744 | tf_op jit(solution)/shard_map/all_gather | solution.py:449
  204.4 6.9 %convolution_convert_fusion.1 = bf16[512,768]{1,0:T(8,128)(2,1)} fusion(bf16[512,3072]{1,0:T(8,128)(2,1)} %all-gather.9.cloned.1.call-done, bf16[3072,768]{1,0:T(8,128)(2,1)} %all-gather.7.cloned.1.call-done), kind=kOutput, calls=%fused_computation.4 | convolution fusion | flops 2416312320 | bytes 8650752 | tf_op jit(solution)/shard_map/dot_general | solution.py:454
  211.2 0.0 copy-start.1
  211.2 0.0 all-to-all-done.4
  211.2 4.5 %all-to-all-start.3 = ((bf16[8,64,768]{2,1,0:T(8,128)(2,1)}), bf16[8,64,768]{2,1,0:T(8,128)(2,1)}, u32[]{:S(2)}, u32[]{:S(2)}) async-start(bf16[8,64,768]{2,1,0:T(8,128)(2,1)} %bitcast.9), calls=%async_computation.3 | async-start | bytes 1572864 | tf_op jit(solution)/shard_map/all_to_all | solution.py:456
  215.8 0.0 copy-done.4
  215.8 0.1 copy.96
  215.9 0.1 eq.98
  216.0 0.1 eq.94
  216.2 0.0 copy-done.3
  216.2 0.6 reduce-window.6
  216.8 0.2 slice_reduce_fusion
  217.1 0.1 fusion.3
  217.2 0.1 reduce_sum.31
  217.3 0.1 copy.98
  217.4 0.7 fusion.2.sel_ref
  218.1 0.1 copy.105
  218.1 18.4 %all-to-all-done.3 = bf16[8,64,768]{2,1,0:T(8,128)(2,1)} async-done(((bf16[8,64,768]{2,1,0:T(8,128)(2,1)}), bf16[8,64,768]{2,1,0:T(8,128)(2,1)}, u32[]{:S(2)}, u32[]{:S(2)}) %all-to-all-start.3) | async-done | bytes 786464 | tf_op jit(solution)/shard_map/all_to_all | solution.py:456
  236.5 1.2 copy.103
  237.7 0.0 copy-done.1
  237.8 2.2 convert_add_fusion
  239.9 0.0 copy-start.2
  239.9 0.6 multiply_convert_fusion.x_ref
  240.5 0.0 copy-start
  240.5 1.1 copy-done
  241.7 0.0 copy-done.2
  241.7 0.5 fusion.5
  242.2 0.2 reduce-precision_convert_fusion
  242.4 0.7 pad_maximum_fusion.1.mix_ref
  243.1 159.7 %experts.1 = bf16[128,6144]{1,0:T(8,128)(2,1)} custom-call(bf16[128,6144]{1,0:T(8,128)(2,1)} %copy-done, bf16[272,128]{1,0:T(8,128)(2,1)} %fusion.2.sel_ref, bf16[256,272]{1,0:T(8,128)(2,1)} %pad_maximum_fusion.1.mix_ref, f32[128,6144]{1,0:T(8,128)} %get-tuple-element.13.stream_ref, bf16[1,6144,1024]{2,1,0:T(8,128)(2,1)} %u_hbm.1, ...), custom_call_target="tpu_custom_call" | custom-call | flops 6845104128 | bytes 25165824 | tf_op jit(solution)/shard_map/experts/pallas_call | solution.py:375
  402.8 2.7 copy.109
  (10 shorter events, 0.1 us)
Async XLA Ops:
  6.5 42.1 %all-gather.5.cloned.1.call-start = ((), (), s32[]{:S(2)}) async-start(), calls=%async_computation.5 | async-start | bytes 2359296 | tf_op jit(solution)/shard_map/all_gather | solution.py:439
  19.6 89.3 %all-gather.7.cloned.1.call-start = ((), (), s32[]{:S(2)}) async-start(), calls=%async_computation.6 | async-start | bytes 5898240 | tf_op jit(solution)/shard_map/all_gather | solution.py:442
  34.3 114.6 %all-gather.11.cloned.1.call-start = ((), (), s32[]{:S(2)}) async-start(), calls=%async_computation.8 | async-start | bytes 3538944 | tf_op jit(solution)/shard_map/all_gather | solution.py:450
  83.0 121.4 %all-gather.9.cloned.1.call-start = ((), (), s32[]{:S(2)}) async-start(), calls=%async_computation.7 | async-start | bytes 3538944 | tf_op jit(solution)/shard_map/all_gather | solution.py:449
  155.6 55.6 %all-to-all-start.4 = ((bf16[8,64,768]{2,1,0:T(8,128)(2,1)}), bf16[8,64,768]{2,1,0:T(8,128)(2,1)S(1)}, u32[]{:S(2)}, u32[]{:S(2)}) async-start(bf16[8,64,768]{2,1,0:T(8,128)(2,1)} %bitcast.11), calls=%async_computation.4 | async-start | bytes 1572864 | tf_op jit(solution)/shard_map/all_to_all | solution.py:456
  159.2 56.6 %copy-start.4 = (s32[128,2]{0,1:T(2,128)S(1)}, s32[128,2]{0,1:T(2,128)}, u32[]{:S(2)}) copy-start(s32[128,2]{0,1:T(2,128)} %param.19) | copy-start | bytes 3076
  159.2 57.0 %copy-start.3 = (bf16[6144]{0:T(1024)(128)(2,1)S(1)}, bf16[6144]{0:T(1024)(128)(2,1)}, u32[]{:S(2)}) copy-start(bf16[6144]{0:T(1024)(128)(2,1)} %param.17) | copy-start | bytes 36868
  211.2 26.5 %copy-start.1 = (bf16[128,6144]{1,0:T(8,128)(2,1)S(1)}, bf16[128,6144]{1,0:T(8,128)(2,1)}, u32[]{:S(2)}) copy-start(bf16[128,6144]{1,0:T(8,128)(2,1)} %param.15) | copy-start | bytes 4718596
  211.2 25.3 %all-to-all-start.3 = ((bf16[8,64,768]{2,1,0:T(8,128)(2,1)}), bf16[8,64,768]{2,1,0:T(8,128)(2,1)}, u32[]{:S(2)}, u32[]{:S(2)}) async-start(bf16[8,64,768]{2,1,0:T(8,128)(2,1)} %bitcast.9), calls=%async_computation.3 | async-start | bytes 1572864 | tf_op jit(solution)/shard_map/all_to_all | solution.py:456
  239.9 1.8 copy-start.2
  240.5 1.1 copy-start
Sparse Core Ops, SparseCore 0:
  19.7 28.8 all-gather.4
  50.5 58.4 all-gather.6
  110.6 38.2 all-gather.10
  150.4 53.9 all-gather.8

commit v2 on v0

v2 whole, which is shorter than its diff:
```python
import functools

import jax
import jax.numpy as jnp
from jax import lax
from jax.experimental import pallas as pl
from jax.experimental.pallas import tpu as pltpu
from jax.sharding import PartitionSpec as P

D = 6144
HEADS = 24
KV_HEADS = 4
HEAD_DIM = 128
EXPERTS = 8
RANK = 512
TOK_DEV = 128
CAP = 33


EPS = 1e-05
LOG2_E = 1.4426950408889634


MAIN = CAP // 16 * 16
PAD = 16
PIECE = 384
AHEAD = 3


def flipped(index, bits):
    bit = 1
    while bit <= bits:
        if bits & bit:
            index = index + bit * (1 - 2 * ((index // bit) % 2))
        bit *= 2
    return index


def at(**place):
    return {"device_id": place, "device_id_type": pl.DeviceIdType.MESH}


def greet(seq_count, exp_count):
    seq, exp = lax.axis_index("seq"), lax.axis_index("exp")
    barrier = pltpu.get_barrier_semaphore()
    for d in range(1, exp_count):
        pl.semaphore_signal(barrier, inc=1, **at(exp=flipped(exp, d)))
    for d in range(1, seq_count):
        for c in range(2):
            pl.semaphore_signal(
                barrier, inc=1, **at(seq=flipped(seq, d), exp=flipped(exp, c))
            )
    return barrier, exp_count - 1 + 2 * (seq_count - 1)


MAIN = CAP // 16 * 16
PAD = 16
PIECE = 384
AHEAD = 3


def flipped(index, bits):
    bit = 1
    while bit <= bits:
        if bits & bit:
            index = index + bit * (1 - 2 * ((index // bit) % 2))
        bit *= 2
    return index


def at(**place):
    return {"device_id": place, "device_id_type": pl.DeviceIdType.MESH}


def greet(seq_count, exp_count):
    seq, exp = lax.axis_index("seq"), lax.axis_index("exp")
    barrier = pltpu.get_barrier_semaphore()
    for d in range(1, exp_count):
        pl.semaphore_signal(barrier, inc=1, **at(exp=flipped(exp, d)))
    for d in range(1, seq_count):
        for c in range(2):
            pl.semaphore_signal(
                barrier, inc=1, **at(seq=flipped(seq, d), exp=flipped(exp, c))
            )
    return barrier, exp_count - 1 + 2 * (seq_count - 1)


def attention_kernel(
    seq_count,
    exp_count,
    q_ref,
    k_ref,
    v_ref,
    w_hbm,
    out_ref,
    near_hbm,
    q_all,
    kv_all,
    in_send,
    in_recv,
    q_send,
    q_recv,
    kv_send,
    kv_recv,
    w_send,
    w_recv,
    out_send,
    out_recv,
):
    seq, exp = lax.axis_index("seq"), lax.axis_index("exp")
    chips = exp_count // 2
    chip, core = exp // 2, exp % 2
    heads = HEADS // seq_count
    width = heads * HEAD_DIM
    shares = max(1, seq_count // KV_HEADS)
    barrier, greetings = greet(seq_count, exp_count)
    own = pl.ds(pl.multiple_of((seq // shares) * HEAD_DIM, HEAD_DIM), HEAD_DIM)
    kv_all[exp, seq, :, :HEAD_DIM] = k_ref[:, own]
    kv_all[exp, seq, :, HEAD_DIM:] = v_ref[:, own]
    q_all[seq] = q_ref[:, pl.ds(pl.multiple_of(seq * width, width), width)]
    pl.semaphore_wait(barrier, greetings)

    def kv_copy(half, peer, block):
        ref = (k_ref, v_ref)[half]
        head = pl.ds(pl.multiple_of((peer // shares) * HEAD_DIM, HEAD_DIM), HEAD_DIM)
        return pltpu.make_async_remote_copy(
            src_ref=ref.at[:, head],
            dst_ref=kv_all.at[exp, block, :, pl.ds(half * HEAD_DIM, HEAD_DIM)],
            send_sem=in_send.at[half, peer],
            recv_sem=in_recv.at[half, block],
            **at(seq=peer),
        )

    def q_copy(peer, block):
        return pltpu.make_async_remote_copy(
            src_ref=q_ref.at[:, pl.ds(pl.multiple_of(peer * width, width), width)],
            dst_ref=q_all.at[block],
            send_sem=q_send.at[peer],
            recv_sem=q_recv.at[block],
            **at(seq=peer),
        )

    for d in range(1, seq_count):
        for half in range(2):
            kv_copy(half, flipped(seq, d), seq).start()
    for d in range(1, seq_count):
        q_copy(flipped(seq, d), seq).start()

    def pass_on(way, block, target):
        return pltpu.make_async_remote_copy(
            src_ref=kv_all.at[block],
            dst_ref=kv_all.at[block],
            send_sem=kv_send.at[way, block],
            recv_sem=kv_recv.at[block],
            **at(exp=target),
        )

    def weight(way, target):
        return pltpu.make_async_remote_copy(
            src_ref=w_hbm,
            dst_ref=near_hbm.at[way],
            send_sem=w_send.at[way],
            recv_sem=w_recv.at[way],
            **at(exp=target),
        )

    partner = flipped(exp, 1)

    def spread(block, up, down, act):
        if up:

            @pl.when(chip + 1 < chips)
            def _():
                act(pass_on(0, block, exp + 2))

        if down:

            @pl.when(chip >= 1)
            def _():
                act(pass_on(1, block, exp - 2))

        act(pass_on(2, block, partner))

    def start(copy):
        copy.start()

    def sent(copy):
        copy.wait_send()

    for d in range(1, seq_count):
        for half in range(2):
            peer = flipped(seq, d)
            kv_copy(half, peer, peer).wait_recv()
    spread(exp, True, True, start)

    def relay(act, wait):
        for hop in range(1, chips):
            below, above = exp - 2 * hop, exp + 2 * hop

            @pl.when(chip >= hop)
            def _():
                if wait:
                    pass_on(2, below, partner).wait_recv()
                spread(below, True, False, act)

            @pl.when(chip + hop < chips)
            def _():
                if wait:
                    pass_on(2, above, partner).wait_recv()
                spread(above, False, True, act)

    relay(start, True)

    @pl.when(chip + 1 < chips)
    def _():
        weight(0, exp + 2).start()

    @pl.when(chip >= 1)
    def _():
        weight(1, exp - 2).start()

    for other in range(chips):
        pass_on(2, 2 * other + 1 - core, partner).wait_recv()
    for d in range(1, seq_count):
        peer = flipped(seq, d)
        q_copy(peer, peer).wait_recv()

    parts = max(1, exp_count * TOK_DEV // 512)
    span = exp_count // parts
    chunk = span * TOK_DEV
    rows = heads * TOK_DEV

    def attend(block, unused):
        query = jnp.concatenate(
            [q_all[block, :, h * HEAD_DIM : (h + 1) * HEAD_DIM] for h in range(heads)], axis=0
        )

        def step(index, carried, masked):
            row_max, row_sum, weighted = carried
            held = kv_all[pl.ds((index % parts) * span, span), index // parts]
            held = held.reshape(chunk, 2 * HEAD_DIM)
            scores = lax.dot_general(
                query,
                held[:, :HEAD_DIM],
                (((1,), (1,)), ((), ())),
                preferred_element_type=jnp.float32,
            ) * (HEAD_DIM ** (-0.5) * LOG2_E)
            if masked:
                offset = (exp % span) * TOK_DEV
                mine = lax.broadcasted_iota(jnp.int32, (rows, chunk), 0) % TOK_DEV + offset
                other = lax.broadcasted_iota(jnp.int32, (rows, chunk), 1)
                scores = jnp.where(other <= mine, scores, -jnp.inf)
            new_max = jnp.maximum(row_max, jnp.max(scores, axis=-1, keepdims=True))
            fading = jnp.exp2(row_max - new_max)
            terms = jnp.exp2(scores - new_max)
            row_sum = row_sum * fading + jnp.sum(terms, axis=-1, keepdims=True)
            update = jnp.dot(
                terms.astype(jnp.bfloat16), held[:, HEAD_DIM:], preferred_element_type=jnp.float32
            )
            return new_max, row_sum, weighted * fading + update

        carried = (
            jnp.full((rows, 1), -1e30, jnp.float32),
            jnp.zeros((rows, 1), jnp.float32),
            jnp.zeros((rows, HEAD_DIM), jnp.float32),
        )
        last = block * parts + exp // span
        carried = lax.fori_loop(0, last, lambda index, now: step(index, now, False), carried)
        row_max, row_sum, weighted = step(last, carried, True)
        result = (weighted / row_sum).astype(jnp.bfloat16)
        for h in range(heads):
            out_ref[core, block, :, h * HEAD_DIM : (h + 1) * HEAD_DIM] = result[
                h * TOK_DEV : (h + 1) * TOK_DEV
            ]
        share(core, block).start()
        return unused

    def share(slot, block):
        return pltpu.make_async_remote_copy(
            src_ref=out_ref.at[slot, block],
            dst_ref=out_ref.at[slot, block],
            send_sem=out_send.at[block],
            recv_sem=out_recv.at[block],
            **at(exp=partner),
        )

    lax.fori_loop(0, seq_count, attend, 0)
    for d in range(1, seq_count):
        peer = flipped(seq, d)
        for half in range(2):
            kv_copy(half, peer, peer).wait_send()
        q_copy(peer, peer).wait_send()
    spread(exp, True, True, sent)
    relay(sent, False)
    for block in range(seq_count):
        share(core, block).wait_send()
        share(1 - core, block).wait_recv()

    @pl.when(chip + 1 < chips)
    def _():
        weight(0, exp + 2).wait_send()
        weight(1, partner).wait_recv()

    @pl.when(chip >= 1)
    def _():
        weight(1, exp - 2).wait_send()
        weight(0, partner).wait_recv()


def attention(queries, keys, values, proj_weight):
    seq_count, exp_count = lax.axis_size("seq"), lax.axis_size("exp")
    width = HEADS // seq_count * HEAD_DIM
    blocks = (seq_count, TOK_DEV, width)
    pairs = HEADS // seq_count * seq_count * TOK_DEV * exp_count * seq_count * TOK_DEV // 2
    vmem = pl.BlockSpec(memory_space=pltpu.VMEM)
    anywhere = pl.BlockSpec(memory_space=pl.ANY)
    dma = pltpu.SemaphoreType.DMA
    return pl.pallas_call(
        functools.partial(attention_kernel, seq_count, exp_count),
        out_shape=(
            jax.ShapeDtypeStruct((2, *blocks), jnp.bfloat16),
            jax.ShapeDtypeStruct((2, *proj_weight.shape), jnp.bfloat16),
        ),
        in_specs=[vmem, vmem, vmem, anywhere],
        out_specs=(vmem, anywhere),
        scratch_shapes=[
            pltpu.VMEM(blocks, jnp.bfloat16),
            pltpu.VMEM((exp_count, seq_count, TOK_DEV, 2 * HEAD_DIM), jnp.bfloat16),
            dma((2, seq_count)),
            dma((2, seq_count)),
            dma((seq_count,)),
            dma((seq_count,)),
            dma((3, exp_count)),
            dma((exp_count,)),
            dma((2,)),
            dma((2,)),
            dma((seq_count,)),
            dma((seq_count,)),
        ],
        compiler_params=pltpu.CompilerParams(
            collective_id=1, has_side_effects=True, vmem_limit_bytes=60 * 1024 * 1024
        ),
        cost_estimate=pl.CostEstimate(
            flops=pairs * 4 * HEAD_DIM, bytes_accessed=queries.size * 4, transcendentals=pairs
        ),
        name="attention",
    )(queries, keys, values, proj_weight)


def gather_lanes(ref, chunk, tiles):
    return jnp.concatenate([ref[chunk, :, t, :] for t in range(tiles)], axis=1)


def padded(rows):
    count = rows.shape[0]
    if count % PAD:
        rows = jnp.concatenate(
            [rows, jnp.zeros((PAD - count % PAD, rows.shape[1]), rows.dtype)], axis=0
        )
    return rows.astype(jnp.bfloat16)


def layer_kernel(
    seq_count,
    count,
    steps,
    depth,
    att_ref,
    res_ref,
    gain_ref,
    router_ref,
    sel_ref,
    first_ref,
    second_ref,
    named_ref,
    w_hbm,
    near_hbm,
    u_hbm,
    vg_hbm,
    ud_hbm,
    vd_hbm,
    out_ref,
    far_hbm,
    w_buf,
    part_send,
    part_recv,
    stream,
    u_buf,
    vg_buf,
    ud_buf,
    send,
    recv,
    back,
    send_x,
    recv_x,
    back_x,
    rank_sum,
    rank_in,
    square,
    token,
    mix_both,
    swap,
    swap_x,
    w_sem,
    load_sem,
    far_send,
    far_recv,
    part_send_sem,
    part_recv_sem,
    send_sem,
    recv_sem,
    send_x_sem,
    recv_x_sem,
    swap_sem,
):
    seq, me = lax.axis_index("seq"), lax.axis_index("exp")
    chips = count // 2
    chip, core = me // 2, me % 2
    pieces = count // EXPERTS
    piece_width = D // pieces
    block = D // count
    sub = block // PIECE
    width = 2 * PIECE
    tiles = width // 128
    total = chips * sub
    local = total // pieces
    unit = vg_buf.shape[-1]
    mine = me % pieces
    early = chip < (chips + 1) // 2
    rows_in = TOK_DEV * 2 * seq_count
    barrier, greetings = greet(seq_count, count)

    def chunk_of(i):
        return jnp.where(early, i, total - 1 - i)

    def columns(g):
        first = (g // sub) * 2 * block + (g % sub) * PIECE
        return first, first + block

    def span(start):
        return pl.ds(pl.multiple_of(start, 128), PIECE)

    def u_copies(l):
        return [
            pltpu.make_async_copy(
                u_hbm.at[0, pl.ds(pl.multiple_of(start - mine * piece_width, 128), PIECE)],
                u_buf.at[l, pl.ds(p * PIECE, PIECE)],
                w_sem.at[p, l],
            )
            for p, start in enumerate(columns(mine * local + l))
        ]

    def vd_copies(l):
        return [
            pltpu.make_async_copy(
                vd_hbm.at[0, :, span(start - mine * piece_width)],
                u_buf.at[l, pl.ds(0, RANK), pl.ds(p * PIECE, PIECE)],
                w_sem.at[2 + p, l],
            )
            for p, start in enumerate(columns(mine * local + l))
        ]

    def vg_copy(f):
        cols = pl.ds(pl.multiple_of(f * unit, unit), unit)
        return pltpu.make_async_copy(vg_hbm.at[0, :, :, cols], vg_buf.at[f % depth], w_sem.at[4, f])

    def ud_copy(f):
        rows = pl.ds(pl.multiple_of(f * unit, unit), unit)
        return pltpu.make_async_copy(ud_hbm.at[0, rows], ud_buf.at[f % depth], w_sem.at[5, f])

    def weight_hop(way, source, origin, h):
        return pltpu.make_async_remote_copy(
            src_ref=source,
            dst_ref=far_hbm.at[origin, h],
            send_sem=far_send.at[way, origin, h],
            recv_sem=far_recv.at[origin, h],
            **at(exp=me + 2 if way == 0 else me - 2),
        )

    inner = (chip >= 1) & (chip + 1 < chips)

    def start(copy):
        copy.start()

    def sent(copy):
        copy.wait_send()

    def near_hops(act):
        @pl.when(inner)
        def _():
            for h in range(sub):
                for way, k in ((0, sub - 1 - h), (1, h)):
                    source = near_hbm.at[way, :, pl.ds(k * PIECE, PIECE)]
                    act(weight_hop(way, source, chip - 1 if way == 0 else chip + 1, k))

    def far_arrival(origin, h):
        return pltpu.make_async_remote_copy(
            src_ref=far_hbm.at[origin, h],
            dst_ref=far_hbm.at[origin, h],
            send_sem=far_send.at[0, origin, h],
            recv_sem=far_recv.at[origin, h],
            **at(exp=flipped(me, 1)),
        )

    def pump(distance, h, act, wait):
        below, above = chip - distance, chip + distance

        @pl.when((below >= 0) & (chip + 1 < chips))
        def _():
            k = sub - 1 - h
            if wait:
                far_arrival(below, k).wait_recv()
            act(weight_hop(0, far_hbm.at[below, k], below, k))

        @pl.when((above < chips) & (chip >= 1))
        def _():
            if wait:
                far_arrival(above, h).wait_recv()
            act(weight_hop(1, far_hbm.at[above, h], above, h))

    pumps = [(distance, h) for distance in range(2, chips - 1) for h in range(sub)]

    def load(i):
        g = chunk_of(i)
        origin, h = g // sub, g % sub
        cols = span(h * PIECE)

        @pl.when(origin == chip)
        def _():
            pltpu.make_async_copy(w_hbm.at[:, cols], w_buf, load_sem).start()

        @pl.when(origin == chip - 1)
        def _():
            pltpu.make_async_copy(near_hbm.at[0, :, cols], w_buf, load_sem).start()

        @pl.when(origin == chip + 1)
        def _():
            pltpu.make_async_copy(near_hbm.at[1, :, cols], w_buf, load_sem).start()

        @pl.when((origin >= chip + 2) | (origin <= chip - 2))
        def _():
            @pl.when(((origin > chip) & (chip == 0)) | ((origin < chip) & (chip == chips - 1)))
            def _():
                far_arrival(origin, h).wait_recv()

            pltpu.make_async_copy(far_hbm.at[origin, h], w_buf, load_sem).start()

        pltpu.make_async_copy(w_hbm.at[:, cols], w_buf, load_sem).wait()

    def part_copy(i, d, t, block_from, core_from):
        peer, exp = flipped(seq, d), flipped(me, t)
        return pltpu.make_async_remote_copy(
            src_ref=part_send.at[i % (AHEAD + 1), exp % 2, peer],
            dst_ref=part_recv.at[i, core_from, block_from],
            send_sem=part_send_sem.at[i % (AHEAD + 1), exp % 2, peer],
            recv_sem=part_recv_sem.at[i, core_from, block_from],
            **at(seq=peer, exp=exp),
        )

    targets = [(d, t) for d in range(seq_count) for t in range(2) if d or t]

    def parts_sent(i):
        for d, t in targets:
            part_copy(i, d, t, seq, core).wait_send()

    def project(i):
        load(i)
        part = jnp.dot(
            att_ref[...].reshape(rows_in, att_ref.shape[-1]),
            w_buf[...],
            preferred_element_type=jnp.float32,
        )
        slot = i % (AHEAD + 1)
        part_send[slot] = part.astype(jnp.bfloat16).reshape(2, seq_count, TOK_DEV, PIECE)
        for d, t in targets:
            part_copy(i, d, t, seq, core).start()
        part_recv[i, core, seq] = part_send[slot, core, seq]

    def copies(phase, l, peer, slot, into, into_x):
        main = pltpu.make_async_remote_copy(
            src_ref=send.at[l, peer],
            dst_ref=into.at[l, slot],
            send_sem=send_sem.at[phase, l, peer],
            recv_sem=recv_sem.at[phase, l, slot],
            **at(exp=peer),
        )
        extra = pltpu.make_async_remote_copy(
            src_ref=send_x.at[l, peer],
            dst_ref=into_x.at[l, slot],
            send_sem=send_x_sem.at[phase, l, peer],
            recv_sem=recv_x_sem.at[phase, l, slot],
            **at(exp=peer),
        )
        return main, extra

    def send_chunk(phase, l, piece, into, into_x):
        for d in range(1, count):
            peer = flipped(me, d)

            def go():
                for copy in copies(phase, l, peer, me, into, into_x):
                    copy.start()

            if piece is None or pieces == 1:
                go()
            else:
                pl.when(peer % pieces == piece)(go)

        def keep():
            into[l, me] = send[l, me]
            into_x[l, me] = send_x[l, me]

        if piece is None or pieces == 1:
            keep()
        else:
            pl.when(mine == piece)(keep)

    def wait_sent(phase, l, into, into_x):
        for d in range(1, count):
            peer = flipped(me, d)
            for copy in copies(phase, l, peer, peer, into, into_x):
                copy.wait_send()

    def wait_got(phase, l, into, into_x, peers):
        for peer in peers:

            @pl.when(peer != me)
            def _():
                for copy in copies(phase, l, peer, peer, into, into_x):
                    copy.wait_recv()

    def finish(i):
        g = chunk_of(i)
        for d, t in targets:
            peer, exp = flipped(seq, d), flipped(me, t)
            part_copy(i, d, t, peer, exp % 2).wait_recv()
        halves = []
        for p, first in enumerate(columns(g)):
            update = part_recv[i, p, 0].astype(jnp.float32)
            for s in range(1, seq_count):
                update = update + part_recv[i, p, s].astype(jnp.float32)
            update = update.astype(jnp.bfloat16).astype(jnp.float32)
            value = res_ref[:, span(first)].astype(jnp.float32) + update
            stream[g, :, p * PIECE : (p + 1) * PIECE] = value
            token[0] += jnp.broadcast_to(
                jnp.sum(value * value, axis=-1, keepdims=True), (TOK_DEV, 128)
            )
            gained = (value * gain_ref[:, span(first)]).astype(jnp.bfloat16)
            token[1, :, :PAD] += lax.dot_general(
                gained,
                router_ref[:, span(first)],
                (((1,), (1,)), ((), ())),
                preferred_element_type=jnp.float32,
            )
            halves.append(value.astype(jnp.bfloat16))
        rows = jnp.dot(
            sel_ref[...], jnp.concatenate(halves, axis=1), preferred_element_type=jnp.float32
        )
        piece, l = g // local, g % local
        for k in range(EXPERTS):
            send[l, k * pieces + piece] = rows[k * MAIN : (k + 1) * MAIN].astype(jnp.bfloat16)
        extra = rows[EXPERTS * MAIN : EXPERTS * MAIN + EXPERTS]
        for t in range(tiles):
            lanes = extra[:, t * 128 : (t + 1) * 128]
            if pieces == 1:
                send_x[l, :, t, :] = lanes
            else:
                for k in range(EXPERTS):
                    send_x[l, k * pieces + piece, t : t + 1, :] = lanes[k : k + 1]
        send_chunk(0, l, piece, recv, recv_x)

    def weights_in():
        for l in range(local):
            for copy in u_copies(l):
                copy.start()
        for f in range(min(depth, steps)):
            vg_copy(f).start()
            ud_copy(f).start()

    pl.semaphore_wait(barrier, greetings)
    near_hops(start)
    weights_in()
    if len(pumps) > 2:
        for distance, h in pumps:
            pump(distance, h, start, True)
    token[...] = jnp.zeros_like(token)
    square[...] = jnp.zeros_like(square)
    rank_sum[...] = jnp.zeros_like(rank_sum)

    def first_half(i, carried):
        @pl.when(i < total)
        def _():
            @pl.when(i > AHEAD)
            def _():
                parts_sent(i - AHEAD - 1)

            project(i)

        @pl.when(i >= AHEAD)
        def _():
            finish(i - AHEAD)

        if len(pumps) <= 2:
            for place, (distance, h) in enumerate(pumps):

                @pl.when(i == AHEAD + 1 + place)
                def _():
                    pump(distance, h, start, True)

        return carried

    lax.fori_loop(0, total + AHEAD, first_half, 0)
    for i in range(total - AHEAD - 1, total):
        parts_sent(i)

    split = 2 * ((chips + 1) // 2)
    main_rows = count * MAIN

    def spread_gain(l):
        return jnp.concatenate(
            [gain_ref[:, span(start)] for start in columns(mine * local + l)], axis=1
        )

    def first_factor(t, carried):
        for low, high, l in ((0, split, t), (split, count, local - 1 - t)):
            wait_got(0, l, recv, recv_x, range(low, high))
            held = recv[l, low:high].reshape((high - low) * MAIN, width).astype(jnp.float32)
            extra = jnp.concatenate([recv_x[l, low:high, k, :] for k in range(tiles)], axis=1)
            fill = [jnp.zeros((low, width), jnp.float32)] if low else []
            rest = PAD - high
            fill += [extra] + ([jnp.zeros((rest, width), jnp.float32)] if rest else [])
            extra = jnp.concatenate(fill, axis=0) if len(fill) > 1 else extra
            rows = jnp.concatenate([held, extra], axis=0)
            squares = jnp.sum(rows * rows, axis=-1, keepdims=True)
            squares = jnp.broadcast_to(squares, (rows.shape[0], 128))
            gained = (rows * spread_gain(l)).astype(jnp.bfloat16)
            product = jnp.dot(gained, u_buf[l], preferred_element_type=jnp.float32)
            size = (high - low) * MAIN
            here = slice(low * MAIN, high * MAIN)
            square[here] += squares[:size]
            square[main_rows:] += squares[size:]
            rank_sum[here] += product[:size]
            rank_sum[main_rows:] += product[size:]
        return carried

    for l in range(local):
        for copy in u_copies(l):
            copy.wait()
    lax.fori_loop(0, local, first_factor, 0)
    for l in range(local):
        for copy in vd_copies(l):
            copy.start()

    def exchange(source, target, slot, bit):
        copy = pltpu.make_async_remote_copy(
            src_ref=source,
            dst_ref=target,
            send_sem=swap_sem.at[slot, 0],
            recv_sem=swap_sem.at[slot, 1],
            **at(exp=flipped(me, bit)),
        )
        copy.start()
        copy.wait()

    def add_pieces(slot, columns, with_square):
        bit = 1
        while bit < pieces:
            swap[slot, 0, :, :columns] = rank_sum[:, :columns].astype(jnp.bfloat16)
            exchange(swap.at[slot, 0], swap.at[slot, 1], 2 * slot, bit)
            rank_sum[:, :columns] += swap[slot, 1, :, :columns].astype(jnp.float32)
            if with_square:
                swap_x[slot, 0] = square[...]
                exchange(swap_x.at[slot, 0], swap_x.at[slot, 1], 2 * slot + 1, bit)
                square[...] += swap_x[slot, 1]
            bit *= 2
            slot += 1
        return slot

    slot = add_pieces(0, 2 * RANK, True)
    scale = lax.rsqrt(square[:, 0:1] * (1.0 / D) + EPS)
    rank_in[...] = (rank_sum[...] * scale).astype(jnp.bfloat16)
    rank_sum[:, :RANK] = jnp.zeros((rank_sum.shape[0], RANK), jnp.float32)

    def middle(f, carried):
        vg_copy(f).wait()
        ud_copy(f).wait()
        place = f % depth
        gate = jnp.dot(rank_in[:, :RANK], vg_buf[place, 0], preferred_element_type=jnp.float32)
        up = jnp.dot(rank_in[:, RANK:], vg_buf[place, 1], preferred_element_type=jnp.float32)
        hidden = (gate / (1.0 + jnp.exp(-gate)) * up).astype(jnp.bfloat16)
        rank_sum[:, :RANK] += jnp.dot(hidden, ud_buf[place], preferred_element_type=jnp.float32)

        @pl.when(f + depth < steps)
        def _():
            vg_copy(f + depth).start()
            ud_copy(f + depth).start()

        return carried

    lax.fori_loop(0, steps, middle, 0)
    add_pieces(slot, RANK, False)
    rank_in[:, :RANK] = rank_sum[:, :RANK].astype(jnp.bfloat16)

    def last_factor(l, carried):
        for copy in vd_copies(l):
            copy.wait()
        wait_sent(0, l, recv, recv_x)
        rows = jnp.dot(
            rank_in[:, :RANK], u_buf[l, :RANK, :width], preferred_element_type=jnp.float32
        )
        for k in range(count):
            send[l, k] = rows[k * MAIN : (k + 1) * MAIN].astype(jnp.bfloat16)
        extra = rows[main_rows : main_rows + count]
        for t in range(tiles):
            send_x[l, :, t, :] = extra[:, t * 128 : (t + 1) * 128]
        send_chunk(1, l, None, back, back_x)
        return carried

    lax.fori_loop(0, local, last_factor, 0)

    logits = token[1, :, :PAD] * lax.rsqrt(token[0, :, 0:1] * (1.0 / D) + EPS)
    first = jnp.sum(logits * named_ref[0], axis=-1, keepdims=True)
    second = jnp.sum(logits * named_ref[1], axis=-1, keepdims=True)
    mix = first_ref[...].astype(jnp.float32) / (1.0 + jnp.exp(second - first)) + second_ref[
        ...
    ].astype(jnp.float32) / (1.0 + jnp.exp(first - second))
    mix_high = mix.astype(jnp.bfloat16)
    mix_both[:TOK_DEV] = mix_high
    mix_both[TOK_DEV:] = (mix - mix_high.astype(jnp.float32)).astype(jnp.bfloat16)

    def combine(l, carried):
        wait_got(1, l, back, back_x, range(count))
        for piece in range(pieces):
            g = piece * local + l
            rows = back[l].reshape(EXPERTS, pieces, MAIN, width)[:, piece]
            extra = gather_lanes(back_x, l, tiles).reshape(EXPERTS, pieces, width)[:, piece]
            rows = jnp.concatenate([rows.reshape(EXPERTS * MAIN, width), padded(extra)], axis=0)
            both = jnp.dot(mix_both[...], rows, preferred_element_type=jnp.float32)
            result = (stream[g] + both[:TOK_DEV] + both[TOK_DEV:]).astype(jnp.bfloat16)
            for p, first in enumerate(columns(g)):
                out_ref[:, span(first)] = result[:, p * PIECE : (p + 1) * PIECE]
        return carried

    lax.fori_loop(0, local, combine, 0)

    def drain(l, carried):
        wait_sent(1, l, back, back_x)
        return carried

    lax.fori_loop(0, local, drain, 0)
    near_hops(sent)
    for distance, h in pumps:
        pump(distance, h, sent, False)


def layer(attended, residual, gain, router, select, first_at, second_at, named, weights):
    proj_weight, near, u_gate_up, v_gate_up, u_down, v_down = weights
    seq_count, count = lax.axis_size("seq"), lax.axis_size("exp")
    pieces = count // EXPERTS
    sub = D // count // PIECE
    total = count // 2 * sub
    local = total // pieces
    width = 2 * PIECE
    units = u_down.shape[1]
    unit = min(1024, units)
    steps = units // unit
    depth = min(5, max(1, steps - 2))
    rows = count * MAIN + PAD
    swaps = max(1, 2 * (pieces.bit_length() - 1))
    depth_in = proj_weight.shape[0]
    vmem = pl.BlockSpec(memory_space=pltpu.VMEM)
    anywhere = pl.BlockSpec(memory_space=pl.ANY)
    dma = pltpu.SemaphoreType.DMA
    half, full = jnp.bfloat16, jnp.float32
    block = (local, count, MAIN, width)
    block_x = (local, count, width // 128, 128)
    many = pieces > 1
    out, _ = pl.pallas_call(
        functools.partial(layer_kernel, seq_count, count, steps, depth),
        out_shape=(
            jax.ShapeDtypeStruct((TOK_DEV, D), half),
            jax.ShapeDtypeStruct((count // 2, sub, depth_in, PIECE), half),
        ),
        in_specs=[vmem] * 8 + [anywhere] * 6,
        out_specs=(vmem, anywhere),
        scratch_shapes=[
            pltpu.VMEM((depth_in, PIECE), half),
            pltpu.VMEM((AHEAD + 1, 2, seq_count, TOK_DEV, PIECE), half),
            pltpu.VMEM((total, 2, seq_count, TOK_DEV, PIECE), half),
            pltpu.VMEM((total, TOK_DEV, width), full),
            pltpu.VMEM((local, width, 2 * RANK), half),
            pltpu.VMEM((depth, 2, RANK, unit), half),
            pltpu.VMEM((depth, unit, RANK), half),
            pltpu.VMEM(block, half),
            pltpu.VMEM(block, half),
            pltpu.VMEM(block, half),
            pltpu.VMEM(block_x, full),
            pltpu.VMEM(block_x, full),
            pltpu.VMEM(block_x, full),
            pltpu.VMEM((rows, 2 * RANK), full),
            pltpu.VMEM((rows, 2 * RANK), half),
            pltpu.VMEM((rows, 128), full),
            pltpu.VMEM((2, TOK_DEV, 128), full),
            pltpu.VMEM((2 * TOK_DEV, select.shape[0]), half),
            pltpu.VMEM((swaps, 2, rows, 2 * RANK) if many else (1, 2, 16, 128), half),
            pltpu.VMEM((swaps, 2, rows, 128) if many else (1, 2, 8, 128), full),
            dma((6, max(local, steps))),
            dma(()),
            dma((2, count // 2, sub)),
            dma((count // 2, sub)),
            dma((AHEAD + 1, 2, seq_count)),
            dma((total, 2, seq_count)),
            dma((2, local, count)),
            dma((2, local, count)),
            dma((2, local, count)),
            dma((2, local, count)),
            dma((2 * swaps, 2)),
        ],
        compiler_params=pltpu.CompilerParams(
            collective_id=0, has_side_effects=True, vmem_limit_bytes=67043328
        ),
        cost_estimate=pl.CostEstimate(
            flops=rows * RANK * units * 6,
            bytes_accessed=units * RANK * 6,
            transcendentals=rows * units,
        ),
        name="layer",
    )(
        attended,
        residual,
        gain,
        router,
        select,
        first_at,
        second_at,
        named,
        proj_weight,
        near,
        u_gate_up,
        v_gate_up,
        u_down,
        v_down,
    )
    return out


def per_device(
    queries,
    keys,
    values,
    residual,
    proj_weight,
    norm_gain,
    router,
    expert_ids,
    u_gate_up,
    v_gate_up,
    u_down,
    v_down,
):
    attended, near = attention(queries, keys, values, proj_weight)
    expert_range = jnp.arange(EXPERTS, dtype=jnp.int32)
    flat_ids = expert_ids.reshape(TOK_DEV * 2)
    member = (flat_ids[:, None] == expert_range[None, :]).astype(jnp.int32)
    slot_of = jnp.sum((jnp.cumsum(member, axis=0) - 1) * member, axis=1)
    dest = jnp.where(
        slot_of < MAIN, flat_ids * MAIN + slot_of, EXPERTS * MAIN + flat_ids + (slot_of - MAIN)
    ).reshape(TOK_DEV, 2)
    places = jnp.arange(EXPERTS * MAIN + PAD, dtype=jnp.int32)
    first_at = (dest[:, 0:1] == places[None, :]).astype(jnp.bfloat16)
    second_at = (dest[:, 1:2] == places[None, :]).astype(jnp.bfloat16)
    select = (
        (dest[:, 0][None, :] == places[:, None]) | (dest[:, 1][None, :] == places[:, None])
    ).astype(jnp.bfloat16)
    named = (expert_ids.T[:, :, None] == jnp.arange(PAD, dtype=jnp.int32)).astype(jnp.float32)
    return layer(
        attended,
        residual,
        norm_gain.astype(jnp.float32)[None, :],
        jnp.pad(router.T, ((0, PAD - EXPERTS), (0, 0))),
        select,
        first_at,
        second_at,
        named,
        (proj_weight, near, u_gate_up, v_gate_up, u_down, v_down),
    )


def solution(mesh):
    in_specs = (
        P(("seq", "exp"), None),
        P(("seq", "exp"), None),
        P(("seq", "exp"), None),
        P(("seq", "exp"), None),
        P("seq", "exp"),
        P(),
        P(),
        P(("seq", "exp"), None),
        P("exp", None, None),
        P("exp", None, None, None),
        P("exp", None, None),
        P("exp", None, None),
    )
    out_specs = P(("seq", "exp"), None)
    return jax.shard_map(
        per_device, mesh=mesh, in_specs=in_specs, out_specs=out_specs, check_vma=False
    )
```

time: 476 us -> 280 us (0.59)
  Pallas kernels: 30.1 us -> 268 us
  waiting for transfers between devices: 232 us -> 0 us
  blocking collectives: 134 us -> 0 us
  matrix products: 30 us -> 0 us
  local copies, waits for them, and re-layouts: 21.6 us -> 5.76 us
  between operations: 13.5 us -> 0.05 us
  starting transfers between devices: 12.7 us -> 0 us
    pallas_call x2, Pallas kernels: 30.1 us -> 268 us  [the longest x1 210 us: layer(): pl.pallas_call(functools.partial(layer_kernel, seq_count, count, steps, d...]
    all_to_all x4 -> x0, blocking collectives: 134 us -> none  [the longest x1 92.8 us: per_device(): lax.all_to_all(send_rows, 'exp', split_axis=0, concat_axis=0, tiled=True)]
    all_gather x4 -> x0, waiting for transfers between devices: 124 us -> none  [the longest x1 45.2 us: per_device(): lax.all_gather(first_half, 'exp', axis=0, tiled=True)]
    all_to_all x3 -> x0, waiting for transfers between devices: 107 us -> none  [the longest x1 87.8 us: per_device(): lax.all_to_all(expert_out.reshape(exp_count, CAP, piece_width), 'exp', sp...]
    dot_general x8 -> x0, matrix products: 30 us -> none  [the longest x2 13.6 us: per_device(): projected = jnp.dot(rows, weight_rows, preferred_element_type=jnp.float32)]
    reshape x4 -> x0, local copies, waits for them, and re-layouts: 12.7 us -> none  [the longest x1 3.28 us: per_device(): expert_rows = dispatched.reshape(exp_count * CAP, piece_width)]
    all_to_all x3 -> x0, starting transfers between devices: 12.5 us -> none  [the longest x2 7.89 us: per_device(): lax.all_to_all(projected.astype(jnp.bfloat16), 'exp', split_axis=0, conca...]
  transfers between devices with their start and end apart: 7 -> 0, of which waited for: 6 -> 0; matrix products, arithmetic and copies ran while one was open for 4% -> 0% of each run, Pallas kernels for 4% -> 0%
where the time goes in v2:
time: 280 us
  Pallas kernels  268 us (96%)
  local copies, waits for them, and re-layouts  5.76 us (2%)
  other arithmetic  5.59 us (2%)
    pallas_call x1, Pallas kernels, layer(): pl.pallas_call(functools.partial(layer_kernel, seq_count, count, steps, d...  210 us
    pallas_call x1, Pallas kernels, attention(): pl.pallas_call(functools.partial(attention_kernel, seq_count, exp_count),...  58.2 us

profile of v2, /device:TPU:0, one launch (start us, length us, event | category | flops | bytes accessed | tf_op | source)
XLA Modules:
  0.0 279.6 jit_solution(9110011454863848924)
XLA Ops:
  0.0 1.3 broadcast_in_dim.6
  1.3 0.8 copy.25
  2.1 0.1 eq.98
  2.2 0.1 eq.94
  2.4 0.6 reduce-window.6
  3.0 0.2 slice_reduce_fusion
  3.2 0.1 fusion.5
  3.3 0.1 reduce_sum.12
  3.5 0.1 copy.27
  3.5 0.7 compare_select_fusion
  4.3 0.6 fusion.3.sel_ref
  4.9 1.4 fusion.4.named_ref
  6.3 0.8 fusion
  7.1 1.6 pad.4.router_ref
  8.7 58.2 %attention.1 = (bf16[2,4,128,768]{3,2,1,0:T(8,128)(2,1)}, bf16[2,768,768]{2,1,0:T(8,128)(2,1)}) custom-call(bf16[128,3072]{1,0:T(8,128)(2,1)} %q_ref.1, bf16[128,512]{1,0:T(8,128)(2,1)} %k_ref.1, bf16[128,512]{1,0:T(8,128)(2,1)} %v_ref.1, bf16[768,768]{1,0:T(8,128)(2,1)} %w_hbm.3), custom_call_target="tpu_custom_call" | custom-call | flops 3221225472 | bytes 1572864 | tf_op jit(solution)/shard_map/attention/pallas_call | solution.py:318
  66.9 210.0 %layer.1 = (bf16[128,6144]{1,0:T(8,128)(2,1)}, bf16[4,2,768,384]{3,2,1,0:T(8,128)(2,1)}) custom-call(bf16[2,4,128,768]{3,2,1,0:T(8,128)(2,1)} %get-tuple-element.8.att_ref, bf16[128,6144]{1,0:T(8,128)(2,1)} %res_ref.1, f32[1,6144]{1,0:T(1,128)} %bitcast.14, bf16[16,6144]{1,0:T(8,128)(2,1)} %pad.4.router_ref, bf16[272,128]{1,0:T(8,128)(2,1)} %fusion.3.sel_ref, ...), custom_call_target="tpu_custom_call" | custom-call | flops 6845104128 | bytes 25165824 | tf_op jit(solution)/shard_map/layer/pallas_call | solution.py:878
  276.9 2.7 copy.31
  (4 shorter events, 0.1 us)

commit v3 on v2

--- a/solution.py
+++ b/solution.py
@@ -155,14 +155,32 @@
             **at(exp=target),
         )
 
-    def weight(way, target):
+    cut_rows = w_hbm.shape[0] // 2
+    sub = w_hbm.shape[1] // PIECE
+
+    def weight(way, target, u):
+        h = sub - 1 - u // 2 if way == 0 else u // 2
+        rows = pl.ds((u % 2) * cut_rows, cut_rows)
         return pltpu.make_async_remote_copy(
-            src_ref=w_hbm,
-            dst_ref=near_hbm.at[way],
-            send_sem=w_send.at[way],
-            recv_sem=w_recv.at[way],
+            src_ref=w_hbm.at[rows, pl.ds(h * PIECE, PIECE)],
+            dst_ref=near_hbm.at[way, h, rows],
+            send_sem=w_send.at[way, u],
+            recv_sem=w_recv.at[way, u],
             **at(exp=target),
         )
+
+    def weights(low, high):
+        @pl.when(chip + 1 < chips)
+        def _():
+            for u in range(low, high):
+                weight(0, exp + 2, u).start()
+
+        @pl.when(chip >= 1)
+        def _():
+            for u in range(low, high):
+                weight(1, exp - 2, u).start()
+
+    weights(0, 1)
 
     partner = flipped(exp, 1)
 
@@ -211,13 +229,7 @@
 
     relay(start, True)
 
-    @pl.when(chip + 1 < chips)
-    def _():
-        weight(0, exp + 2).start()
-
-    @pl.when(chip >= 1)
-    def _():
-        weight(1, exp - 2).start()
+    weights(1, 2 * sub)
 
     for other in range(chips):
         pass_on(2, 2 * other + 1 - core, partner).wait_recv()
@@ -298,13 +310,15 @@
 
     @pl.when(chip + 1 < chips)
     def _():
-        weight(0, exp + 2).wait_send()
-        weight(1, partner).wait_recv()
+        for u in range(2 * sub):
+            weight(0, exp + 2, u).wait_send()
+            weight(1, partner, u).wait_recv()
 
     @pl.when(chip >= 1)
     def _():
-        weight(1, exp - 2).wait_send()
-        weight(0, partner).wait_recv()
+        for u in range(2 * sub):
+            weight(1, exp - 2, u).wait_send()
+            weight(0, partner, u).wait_recv()
 
 
 def attention(queries, keys, values, proj_weight):
@@ -319,7 +333,9 @@
         functools.partial(attention_kernel, seq_count, exp_count),
         out_shape=(
             jax.ShapeDtypeStruct((2, *blocks), jnp.bfloat16),
-            jax.ShapeDtypeStruct((2, *proj_weight.shape), jnp.bfloat16),
+            jax.ShapeDtypeStruct(
+                (2, proj_weight.shape[1] // PIECE, proj_weight.shape[0], PIECE), jnp.bfloat16
+            ),
         ),
         in_specs=[vmem, vmem, vmem, anywhere],
         out_specs=(vmem, anywhere),
@@ -332,8 +348,8 @@
             dma((seq_count,)),
             dma((3, exp_count)),
             dma((exp_count,)),
-            dma((2,)),
-            dma((2,)),
+            dma((2, proj_weight.shape[1] // PIECE * 2)),
+            dma((2, proj_weight.shape[1] // PIECE * 2)),
             dma((seq_count,)),
             dma((seq_count,)),
         ],
@@ -468,84 +484,86 @@
         rows = pl.ds(pl.multiple_of(f * unit, unit), unit)
         return pltpu.make_async_copy(ud_hbm.at[0, rows], ud_buf.at[f % depth], w_sem.at[5, f])
 
-    def weight_hop(way, source, origin, h):
+    cut_rows = w_hbm.shape[0] // 2
+    units = 2 * sub
+
+    def part_of(way, u):
+        h = sub - 1 - u // 2 if way == 0 else u // 2
+        return h, pl.ds((u % 2) * cut_rows, cut_rows), u % 2
+
+    def weight_hop(way, origin, u, near):
+        h, rows, r = part_of(way, u)
+        target = far_hbm.at[origin, h, rows]
         return pltpu.make_async_remote_copy(
-            src_ref=source,
-            dst_ref=far_hbm.at[origin, h],
-            send_sem=far_send.at[way, origin, h],
-            recv_sem=far_recv.at[origin, h],
+            src_ref=near_hbm.at[way, h, rows] if near else target,
+            dst_ref=target,
+            send_sem=far_send.at[way, origin, h, r],
+            recv_sem=far_recv.at[origin, h, r],
             **at(exp=me + 2 if way == 0 else me - 2),
         )
 
-    inner = (chip >= 1) & (chip + 1 < chips)
+    def far_arrival(origin, h, r):
+        target = far_hbm.at[origin, h, pl.ds(r * cut_rows, cut_rows)]
+        return pltpu.make_async_remote_copy(
+            src_ref=target,
+            dst_ref=target,
+            send_sem=far_send.at[0, origin, h, r],
+            recv_sem=far_recv.at[origin, h, r],
+            **at(exp=flipped(me, 1)),
+        )
+
+    def pump(j, act, wait):
+        distance, u = j // units, j % units
+        below, above = chip - distance, chip + distance
+
+        @pl.when((below >= 0) & (chip + 1 < chips))
+        def _():
+            if wait and distance > 1:
+                h, _, r = part_of(0, u)
+                far_arrival(below, h, r).wait_recv()
+            act(weight_hop(0, below, u, distance == 1))
+
+        @pl.when((above < chips) & (chip >= 1))
+        def _():
+            if wait and distance > 1:
+                h, _, r = part_of(1, u)
+                far_arrival(above, h, r).wait_recv()
+            act(weight_hop(1, above, u, distance == 1))
+
+    pump_count = (chips - 1) * units
 
     def start(copy):
         copy.start()
 
     def sent(copy):
         copy.wait_send()
-
-    def near_hops(act):
-        @pl.when(inner)
-        def _():
-            for h in range(sub):
-                for way, k in ((0, sub - 1 - h), (1, h)):
-                    source = near_hbm.at[way, :, pl.ds(k * PIECE, PIECE)]
-                    act(weight_hop(way, source, chip - 1 if way == 0 else chip + 1, k))
-
-    def far_arrival(origin, h):
-        return pltpu.make_async_remote_copy(
-            src_ref=far_hbm.at[origin, h],
-            dst_ref=far_hbm.at[origin, h],
-            send_sem=far_send.at[0, origin, h],
-            recv_sem=far_recv.at[origin, h],
-            **at(exp=flipped(me, 1)),
-        )
-
-    def pump(distance, h, act, wait):
-        below, above = chip - distance, chip + distance
-
-        @pl.when((below >= 0) & (chip + 1 < chips))
-        def _():
-            k = sub - 1 - h
-            if wait:
-                far_arrival(below, k).wait_recv()
-            act(weight_hop(0, far_hbm.at[below, k], below, k))
-
-        @pl.when((above < chips) & (chip >= 1))
-        def _():
-            if wait:
-                far_arrival(above, h).wait_recv()
-            act(weight_hop(1, far_hbm.at[above, h], above, h))
-
-    pumps = [(distance, h) for distance in range(2, chips - 1) for h in range(sub)]
 
     def load(i):
         g = chunk_of(i)
         origin, h = g // sub, g % sub
-        cols = span(h * PIECE)
 
         @pl.when(origin == chip)
         def _():
-            pltpu.make_async_copy(w_hbm.at[:, cols], w_buf, load_sem).start()
+            pltpu.make_async_copy(w_hbm.at[:, span(h * PIECE)], w_buf, load_sem).start()
 
         @pl.when(origin == chip - 1)
         def _():
-            pltpu.make_async_copy(near_hbm.at[0, :, cols], w_buf, load_sem).start()
+            pltpu.make_async_copy(near_hbm.at[0, h], w_buf, load_sem).start()
 
         @pl.when(origin == chip + 1)
         def _():
-            pltpu.make_async_copy(near_hbm.at[1, :, cols], w_buf, load_sem).start()
+            pltpu.make_async_copy(near_hbm.at[1, h], w_buf, load_sem).start()
 
         @pl.when((origin >= chip + 2) | (origin <= chip - 2))
         def _():
             @pl.when(((origin > chip) & (chip == 0)) | ((origin < chip) & (chip == chips - 1)))
             def _():
-                far_arrival(origin, h).wait_recv()
+                for r in range(2):
+                    far_arrival(origin, h, r).wait_recv()
 
             pltpu.make_async_copy(far_hbm.at[origin, h], w_buf, load_sem).start()
 
-        pltpu.make_async_copy(w_hbm.at[:, cols], w_buf, load_sem).wait()
+        pltpu.make_async_copy(near_hbm.at[0, h], w_buf, load_sem).wait()
 
     def part_copy(i, d, t, block_from, core_from):
         peer, exp = flipped(seq, d), flipped(me, t)
@@ -646,7 +664,7 @@
                 jnp.sum(value * value, axis=-1, keepdims=True), (TOK_DEV, 128)
             )
             gained = (value * gain_ref[:, span(first)]).astype(jnp.bfloat16)
-            token[1, :, :PAD] += lax.dot_general(
+            token[1, :, :EXPERTS] += lax.dot_general(
                 gained,
                 router_ref[:, span(first)],
                 (((1,), (1,)), ((), ())),
@@ -678,11 +696,13 @@
             ud_copy(f).start()
 
     pl.semaphore_wait(barrier, greetings)
-    near_hops(start)
-    weights_in()
-    if len(pumps) > 2:
-        for distance, h in pumps:
-            pump(distance, h, start, True)
+    for j in range(units, 2 * units):
+        pump(j, start, True)
+    rest = list(range(2 * units, pump_count))
+    if len(rest) > 4:
+        for j in rest:
+            pump(j, start, True)
+        rest = []
     token[...] = jnp.zeros_like(token)
     square[...] = jnp.zeros_like(square)
     rank_sum[...] = jnp.zeros_like(rank_sum)
@@ -696,16 +716,18 @@
 
             project(i)
 
+        @pl.when(i == min(AHEAD, total - 1))
+        def _():
+            weights_in()
+
+        @pl.when(i == AHEAD)
+        def _():
+            for j in rest:
+                pump(j, start, True)
+
         @pl.when(i >= AHEAD)
         def _():
             finish(i - AHEAD)
-
-        if len(pumps) <= 2:
-            for place, (distance, h) in enumerate(pumps):
-
-                @pl.when(i == AHEAD + 1 + place)
-                def _():
-                    pump(distance, h, start, True)
 
         return carried
 
@@ -818,7 +840,7 @@
 
     lax.fori_loop(0, local, last_factor, 0)
 
-    logits = token[1, :, :PAD] * lax.rsqrt(token[0, :, 0:1] * (1.0 / D) + EPS)
+    logits = token[1, :, :EXPERTS] * lax.rsqrt(token[0, :, 0:1] * (1.0 / D) + EPS)
     first = jnp.sum(logits * named_ref[0], axis=-1, keepdims=True)
     second = jnp.sum(logits * named_ref[1], axis=-1, keepdims=True)
     mix = first_ref[...].astype(jnp.float32) / (1.0 + jnp.exp(second - first)) + second_ref[
@@ -848,9 +870,8 @@
         return carried
 
     lax.fori_loop(0, local, drain, 0)
-    near_hops(sent)
-    for distance, h in pumps:
-        pump(distance, h, sent, False)
+    for j in range(units, pump_count):
+        pump(j, sent, False)
 
 
 def layer(attended, residual, gain, router, select, first_at, second_at, named, weights):
@@ -906,8 +927,8 @@
             pltpu.VMEM((swaps, 2, rows, 128) if many else (1, 2, 8, 128), full),
             dma((6, max(local, steps))),
             dma(()),
-            dma((2, count // 2, sub)),
-            dma((count // 2, sub)),
+            dma((2, count // 2, sub, 2)),
+            dma((count // 2, sub, 2)),
             dma((AHEAD + 1, 2, seq_count)),
             dma((total, 2, seq_count)),
             dma((2, local, count)),
@@ -960,24 +981,28 @@
 ):
     attended, near = attention(queries, keys, values, proj_weight)
     expert_range = jnp.arange(EXPERTS, dtype=jnp.int32)
-    flat_ids = expert_ids.reshape(TOK_DEV * 2)
-    member = (flat_ids[:, None] == expert_range[None, :]).astype(jnp.int32)
-    slot_of = jnp.sum((jnp.cumsum(member, axis=0) - 1) * member, axis=1)
-    dest = jnp.where(
-        slot_of < MAIN, flat_ids * MAIN + slot_of, EXPERTS * MAIN + flat_ids + (slot_of - MAIN)
-    ).reshape(TOK_DEV, 2)
+    member = (expert_ids[:, :, None] == expert_range).astype(jnp.bfloat16)
+    tokens = jnp.arange(TOK_DEV, dtype=jnp.int32)
+    before = jnp.dot(
+        (tokens[:, None] > tokens[None, :]).astype(jnp.bfloat16),
+        member[:, 0] + member[:, 1],
+        preferred_element_type=jnp.float32,
+    )
+    slot = jnp.sum(member.astype(jnp.float32) * before[:, None, :], axis=-1).astype(jnp.int32)
+    past = expert_ids + (EXPERTS * MAIN - MAIN) + slot
+    dest = jnp.where(slot < MAIN, expert_ids * MAIN + slot, past)
     places = jnp.arange(EXPERTS * MAIN + PAD, dtype=jnp.int32)
     first_at = (dest[:, 0:1] == places[None, :]).astype(jnp.bfloat16)
     second_at = (dest[:, 1:2] == places[None, :]).astype(jnp.bfloat16)
     select = (
         (dest[:, 0][None, :] == places[:, None]) | (dest[:, 1][None, :] == places[:, None])
     ).astype(jnp.bfloat16)
-    named = (expert_ids.T[:, :, None] == jnp.arange(PAD, dtype=jnp.int32)).astype(jnp.float32)
+    named = (expert_ids.T[:, :, None] == expert_range).astype(jnp.float32)
     return layer(
         attended,
         residual,
         norm_gain.astype(jnp.float32)[None, :],
-        jnp.pad(router.T, ((0, PAD - EXPERTS), (0, 0))),
+        router.T,
         select,
         first_at,
         second_at,

time: 280 us -> 269 us (0.961)
  Pallas kernels: 268 us -> 258 us
  local copies, waits for them, and re-layouts: 5.76 us -> 2.7 us
    pallas_call x1, Pallas kernels: 210 us -> 203 us  [layer(): pl.pallas_call(functools.partial(layer_kernel, seq_count, count, steps, d...]
    pallas_call x1, Pallas kernels: 58.2 us -> 55.4 us  [attention(): pl.pallas_call(functools.partial(attention_kernel, seq_count, exp_count),...]
where the time goes in v3:
time: 269 us; the launch traced here: 268 us
  Pallas kernels  258 us (96%)
  other arithmetic  6.27 us (2%)
  local copies, waits for them, and re-layouts  2.7 us (1%)
    pallas_call x1, Pallas kernels, layer(): pl.pallas_call(functools.partial(layer_kernel, seq_count, count, steps, d...  203 us
    pallas_call x1, Pallas kernels, attention(): pl.pallas_call(functools.partial(attention_kernel, seq_count, exp_count),...  55.4 us

profile of v3, /device:TPU:0, one launch (start us, length us, event | category | flops | bytes accessed | tf_op | source)
XLA Modules:
  0.0 267.6 jit_solution(2873102057104773486)
XLA Ops:
  0.0 0.7 fusion.6
  0.7 0.1 fusion.5
  0.8 0.7 multiply_reduce_fusion
  1.5 0.7 compare_select_fusion
  2.2 1.3 broadcast_in_dim.6
  3.6 0.6 fusion.3.sel_ref
  4.2 1.4 fusion.4.named_ref
  5.6 0.8 fusion
  6.4 55.4 %attention.1 = (bf16[2,4,128,768]{3,2,1,0:T(8,128)(2,1)}, bf16[2,2,768,384]{3,2,1,0:T(8,128)(2,1)}) custom-call(bf16[128,3072]{1,0:T(8,128)(2,1)} %q_ref.1, bf16[128,512]{1,0:T(8,128)(2,1)} %k_ref.1, bf16[128,512]{1,0:T(8,128)(2,1)} %v_ref.1, bf16[768,768]{1,0:T(8,128)(2,1)} %w_hbm.3), custom_call_target="tpu_custom_call" | custom-call | flops 3221225472 | bytes 1572864 | tf_op jit(solution)/shard_map/attention/pallas_call | solution.py:332
  61.8 203.1 %layer.1 = (bf16[128,6144]{1,0:T(8,128)(2,1)}, bf16[4,2,768,384]{3,2,1,0:T(8,128)(2,1)}) custom-call(bf16[2,4,128,768]{3,2,1,0:T(8,128)(2,1)} %get-tuple-element.8.att_ref, bf16[128,6144]{1,0:T(8,128)(2,1)} %res_ref.1, f32[1,6144]{1,0:T(1,128)} %bitcast.11, bf16[8,6144]{1,0:T(8,128)(2,1)} %bitcast.10, bf16[272,128]{1,0:T(8,128)(2,1)} %fusion.3.sel_ref, ...), custom_call_target="tpu_custom_call" | custom-call | flops 6845104128 | bytes 25165824 | tf_op jit(solution)/shard_map/layer/pallas_call | solution.py:899
  264.9 2.7 %copy.16 = bf16[128,6144]{1,0:T(8,128)(2,1)} copy(bf16[128,6144]{1,0:T(8,128)(2,1)} %get-tuple-element.10) | data formatting | bytes 3145728
  (1 shorter events, 0.0 us)

commit v4 on v3

--- a/solution.py
+++ b/solution.py
@@ -24,7 +24,7 @@
 MAIN = CAP // 16 * 16
 PAD = 16
 PIECE = 384
-AHEAD = 3
+AHEAD = 2
 
 
 def flipped(index, bits):
@@ -56,7 +56,7 @@
 MAIN = CAP // 16 * 16
 PAD = 16
 PIECE = 384
-AHEAD = 3
+AHEAD = 2
 
 
 def flipped(index, bits):

time: 269 us -> 264 us (0.981)
  Pallas kernels: 258 us -> 254 us
    pallas_call x1, Pallas kernels: 203 us -> 199 us  [layer(): pl.pallas_call(functools.partial(layer_kernel, seq_count, count, steps, d...]
where the time goes in v4:
time: 264 us; the launch traced here: 263 us
  Pallas kernels  254 us (96%)
  other arithmetic  6.27 us (2%)
  local copies, waits for them, and re-layouts  2.7 us (1%)
    pallas_call x1, Pallas kernels, layer(): pl.pallas_call(functools.partial(layer_kernel, seq_count, count, steps, d...  199 us
    pallas_call x1, Pallas kernels, attention(): pl.pallas_call(functools.partial(attention_kernel, seq_count, exp_count),...  55.4 us

profile of v4, /device:TPU:0, one launch (start us, length us, event | category | flops | bytes accessed | tf_op | source)
XLA Modules:
  0.0 263.1 jit_solution(11856738215770907355)
XLA Ops:
  0.0 0.7 fusion.6
  0.7 0.1 fusion.5
  0.8 0.7 multiply_reduce_fusion
  1.5 0.7 compare_select_fusion
  2.2 1.3 broadcast_in_dim.6
  3.6 0.6 fusion.3.sel_ref
  4.2 1.4 fusion.4.named_ref
  5.6 0.8 fusion
  6.4 55.4 %attention.1 = (bf16[2,4,128,768]{3,2,1,0:T(8,128)(2,1)}, bf16[2,2,768,384]{3,2,1,0:T(8,128)(2,1)}) custom-call(bf16[128,3072]{1,0:T(8,128)(2,1)} %q_ref.1, bf16[128,512]{1,0:T(8,128)(2,1)} %k_ref.1, bf16[128,512]{1,0:T(8,128)(2,1)} %v_ref.1, bf16[768,768]{1,0:T(8,128)(2,1)} %w_hbm.3), custom_call_target="tpu_custom_call" | custom-call | flops 3221225472 | bytes 1572864 | tf_op jit(solution)/shard_map/attention/pallas_call | solution.py:332
  61.8 198.6 %layer.1 = (bf16[128,6144]{1,0:T(8,128)(2,1)}, bf16[4,2,768,384]{3,2,1,0:T(8,128)(2,1)}) custom-call(bf16[2,4,128,768]{3,2,1,0:T(8,128)(2,1)} %get-tuple-element.8.att_ref, bf16[128,6144]{1,0:T(8,128)(2,1)} %res_ref.1, f32[1,6144]{1,0:T(1,128)} %bitcast.11, bf16[8,6144]{1,0:T(8,128)(2,1)} %bitcast.10, bf16[272,128]{1,0:T(8,128)(2,1)} %fusion.3.sel_ref, ...), custom_call_target="tpu_custom_call" | custom-call | flops 6845104128 | bytes 25165824 | tf_op jit(solution)/shard_map/layer/pallas_call | solution.py:899
  260.4 2.7 %copy.16 = bf16[128,6144]{1,0:T(8,128)(2,1)} copy(bf16[128,6144]{1,0:T(8,128)(2,1)} %get-tuple-element.10) | data formatting | bytes 3145728
  (1 shorter events, 0.0 us)
